TPU v7x, 256 devices: a whole 4x4x8 slice. The times are simulated.
256 devices in a mesh: gx: 16 (over z, core), gy: 16 (over x, y).
Axes of the slice: x: 4, y: 4, z: 8, core: 2. Of those that a mesh axis runs over, the one named last changes fastest.
Arguments:
- tokens: bfloat16 [4096, 4096], P('gx', 'gy'), may hold values from -6 to 6
- gate_blocks: bfloat16 [16, 16, 10, 128, 128], P('gy', 'gx'), may hold values from -0.125 to 0.125
- up_blocks: bfloat16 [16, 16, 10, 128, 128], P('gy', 'gx'), may hold values from -0.125 to 0.125
- gate_coords: int32 [16, 16, 10, 2], P('gy', 'gx'), may hold values from 0 to 6, as said below
- gate_count: int32 [16, 16], P('gy', 'gx'), may hold values from 3 to 10, as said below
- down_blocks: bfloat16 [16, 16, 6, 128, 128], P('gx', 'gy'), may hold values from -0.09375 to 0.09375
- down_rows: int32 [16, 16, 4], P('gx'), may hold values from 0 to 6, as said below
- down_coords: int32 [16, 16, 6, 2], P('gx', 'gy'), may hold values from 0 to 3, as said below
- down_count: int32 [16, 16], P('gx', 'gy'), may hold values from 2 to 6, as said below
Outputs:
- mixed: bfloat16 [4096, 4096], P('gx', 'gy')
Inputs may be any that keep to these rules, and one draw needn't show every extreme that they name: `gate_coords`: within each tile the 10 (model-width block, hidden block) pairs are distinct, the first below 2, the second below 7; only the first gate_count slots are live. `gate_count`: some tile has all 10 slots live. `down_rows`: within each down tile the 4 hidden blocks are distinct. `down_coords`: within each down tile the 6 (kept-row index below 4, model-width block below 2) pairs are distinct; only the first down_count slots are live. `down_count`: some tile has all 6 slots live.
All inputs are finite; a program needn't handle non-finite values.
Results may differ from a plain program's by a relative error of at most 0.025.
Values may be sent and summed in bfloat16 or wider, within the bound.
A program may use at most 64 MiB of HBM per device.

v0:
```python
import jax
import jax.numpy as jnp
from jax import lax
from jax.sharding import PartitionSpec as P

FF = 14336
BLOCK = 128


def cut_along(value, dim, count):
    shape = value.shape
    parts = value.reshape(*shape[:dim], count, shape[dim] // count, *shape[dim + 1 :])
    return jnp.moveaxis(parts, dim, 0)


def piece_ends(length, count):
    hop = length // count
    if hop >= 8:
        hop -= hop % 8
    return [hop * k for k in range(1, count)]


def in_order(parts, dim):
    parts = jnp.moveaxis(parts, 0, dim)
    shape = parts.shape
    return parts.reshape(*shape[:dim], shape[dim] * shape[dim + 1], *shape[dim + 2 :])


def cut_exchange(value, axis, pieces, split_dim, concat_dim):
    parts = cut_along(value, split_dim, lax.axis_size(axis))
    split_at = max(range(1, max(2, parts.ndim - 1)), key=lambda d: parts.shape[d])
    done = []
    for section in jnp.split(parts, piece_ends(parts.shape[split_at], pieces), axis=split_at):
        if section.size:
            done.append(lax.all_to_all(section, axis, split_axis=0, concat_axis=0, tiled=True))
    return in_order(jnp.concatenate(done, axis=split_at), concat_dim)


def tile_dense(blocks, coords, count, row_count, col_count):
    live = (jnp.arange(coords.shape[0]) < count).astype(jnp.bfloat16)
    pick = jax.nn.one_hot(coords[:, 0], row_count, dtype=jnp.bfloat16)
    place = jax.nn.one_hot(coords[:, 1], col_count, dtype=jnp.bfloat16) * live[:, None]
    dense = jnp.einsum(
        "sr,sc,skm->rkcm", pick, place, blocks, preferred_element_type=jnp.float32
    ).astype(jnp.bfloat16)
    return dense.reshape(row_count * blocks.shape[1], col_count * blocks.shape[2])


def body(
    tokens,
    gate_blocks,
    up_blocks,
    gate_coords,
    gate_count,
    down_blocks,
    down_rows,
    down_coords,
    down_count,
):
    n_model = tokens.shape[1] // BLOCK
    n_hidden = FF // (BLOCK * lax.axis_size("gx"))
    paired_blocks = jnp.concatenate([gate_blocks[:, 0], up_blocks[:, 0]], -1)
    gathered = lax.all_gather(tokens, "gx", axis=0, tiled=True)
    tok_rows = gathered.shape[0] // lax.axis_size("gy")
    dense_pair = tile_dense(
        paired_blocks[0], gate_coords[0, 0], gate_count[0, 0], n_model, n_hidden
    )
    summed = lax.psum_scatter(
        jnp.dot(gathered, dense_pair, preferred_element_type=jnp.float32).astype(jnp.bfloat16),
        "gy",
        scatter_dimension=0,
        tiled=True,
    ).astype(jnp.float32)
    summed = summed.reshape(tok_rows, n_hidden, 2, BLOCK)
    hidden = (jax.nn.silu(summed[:, :, 0]) * summed[:, :, 1]).astype(jnp.bfloat16)
    kept_count = down_rows.shape[-1]
    dense_down = tile_dense(
        down_blocks[0, 0], down_coords[0, 0], down_count[0, 0], kept_count, n_model
    )
    select_every = jax.nn.one_hot(down_rows[0], n_hidden, dtype=jnp.bfloat16)
    outgoing = jnp.einsum(
        "nfk,guf->gnuk", hidden, select_every, preferred_element_type=jnp.float32
    ).astype(jnp.bfloat16)
    outgoing = outgoing.reshape(outgoing.shape[0], tok_rows, kept_count * BLOCK)
    received = cut_exchange(outgoing, "gy", 2, 0, 0)
    kept_all = received.reshape(received.shape[0] * tok_rows, kept_count * BLOCK)
    partial_out = jnp.dot(kept_all, dense_down, preferred_element_type=jnp.float32)
    return lax.psum_scatter(partial_out.astype(jnp.bfloat16), "gx", scatter_dimension=0, tiled=True)


def solution(mesh):
    return jax.shard_map(
        body,
        mesh=mesh,
        in_specs=(
            P("gx", "gy"),
            P("gy", "gx", None, None, None),
            P("gy", "gx", None, None, None),
            P("gy", "gx", None, None),
            P("gy", "gx"),
            P("gx", "gy", None, None, None),
            P("gx", None, None),
            P("gx", "gy", None, None),
            P("gx", "gy"),
        ),
        out_specs=P("gx", "gy"),
        check_vma=False,
    )
```

profile of v0, /device:TPU:6, one launch (start us, length us, event | category | flops | bytes accessed | tf_op | source)
XLA Modules:
  0.0 320.3 jit_solution(4454195248453779331)
XLA Ops:
  6.5 0.0 all-gather.2.cloned.1.call-start
  6.5 0.7 all-gather.2.cloned.1.call-update
  7.3 0.0 reduce-scatter.3.cloned.1.call-start
  8.0 0.8 slice_bitcast_fusion.5
  8.7 1.5 copy_bitcast_fusion
  10.3 0.4 convolution_convert_fusion.2
  10.7 0.3 copy.50
  11.0 40.6 %all-gather.2.cloned.1.call-done = bf16[4096,256]{1,0:T(8,128)(2,1)} async-done(((bf16[256,256]{1,0:T(8,128)(2,1)}), bf16[4096,256]{1,0:T(8,128)(2,1)}) %all-gather.2.cloned.1.call-update) | async-done | bytes 2097168 | tf_op jit(solution)/shard_map/all_gather | solution.py:63
  51.5 8.9 %fusion = bf16[4096,1792]{0,1:T(8,128)(2,1)} fusion(bf16[256,1792]{1,0:T(8,128)(2,1)S(1)} %bitcast.95, bf16[4096,256]{1,0:T(8,128)(2,1)} %all-gather.2.cloned.1.call-done), kind=kOutput, calls=%fused_computation.1 | convolution fusion | flops 3765436416 | bytes 17694720 | tf_op jit(solution)/shard_map/dot_general | solution.py:69
  60.5 0.0 reduce-scatter.3.cloned.1.call-update
  60.5 105.2 %reduce-scatter.3.cloned.1.call-done = bf16[256,1792]{0,1:T(8,128)(2,1)} async-done(((bf16[4096,1792]{0,1:T(8,128)(2,1)}), bf16[256,1792]{0,1:T(8,128)(2,1)}) %reduce-scatter.3.cloned.1.call-update) | async-done | bytes 917520 | tf_op jit(solution)/shard_map/reduce_scatter | solution.py:68
  165.7 1.3 fusion.31
  167.0 0.0 copy-start.1
  167.0 0.4 copy.48
  167.4 0.4 copy.49
  167.9 0.0 copy-done.1
  167.9 3.0 convert_bitcast_fusion
  170.8 7.5 %copy.37 = bf16[16,256,4,128]{1,3,2,0:T(8,128)(2,1)} copy(bf16[16,256,4,128]{3,0,1,2:T(8,128)(2,1)} %convert_bitcast_fusion) | data formatting | bytes 8388608 | tf_op jit(solution)/shard_map/convert_element_type | solution.py:83
  178.3 4.0 %slice_bitcast_fusion.1 = (bf16[16,1,128,512]{2,3,1,0:T(8,128)(2,1)S(1)}, bf16[16,1,128,512]{2,3,1,0:T(8,128)(2,1)}) fusion(bf16[16,1,256,512]{2,3,0,1:T(8,128)(2,1)} %bitcast.94), kind=kLoop, calls=%fused_computation.6 | loop fusion | bytes 8388608 | tf_op jit(solution)/shard_map/split | solution.py:33
  182.3 31.6 %all_to_all.10 = bf16[16,1,128,512]{2,3,1,0:T(8,128)(2,1)} all-to-all(bf16[16,1,128,512]{2,3,1,0:T(8,128)(2,1)S(1)} %get-tuple-element.5), channel_id=1, replica_groups=mesh['gx'=16,'gy'=16] {'gy'}, dimensions={0} | all-to-all | bytes 4194304 | tf_op jit(solution)/shard_map/all_to_all | solution.py:35
  213.9 5.8 %all-to-all-start.1 = ((bf16[16,1,128,512]{2,3,1,0:T(8,128)(2,1)}), bf16[16,1,128,512]{2,3,1,0:T(8,128)(2,1)S(1)}, u32[]{:S(2)}, u32[]{:S(2)}) async-start(bf16[16,1,128,512]{2,3,1,0:T(8,128)(2,1)} %get-tuple-element.6), calls=%async_computation.2 | async-start | bytes 4194304 | tf_op jit(solution)/shard_map/all_to_all | solution.py:35
  219.8 0.0 reduce-scatter.5.cloned.1.call-start
  220.5 0.0 copy-done.2
  220.5 0.2 fusion.1
  220.8 0.3 copy.43
  221.1 3.9 %copy.40 = bf16[16,1,128,512]{3,2,0,1:T(8,128)(2,1)} copy(bf16[16,1,128,512]{2,3,1,0:T(8,128)(2,1)} %all_to_all.10) | data formatting | bytes 4194304 | tf_op jit(solution)/shard_map/all_to_all | solution.py:35
  225.0 20.9 %all-to-all-done.1 = bf16[16,1,128,512]{2,3,1,0:T(8,128)(2,1)S(1)} async-done(((bf16[16,1,128,512]{2,3,1,0:T(8,128)(2,1)}), bf16[16,1,128,512]{2,3,1,0:T(8,128)(2,1)S(1)}, u32[]{:S(2)}, u32[]{:S(2)}) %all-to-all-start.1) | async-done | bytes 2097184 | tf_op jit(solution)/shard_map/all_to_all | solution.py:35
  245.9 2.6 copy.41
  248.5 2.6 pad_maximum_fusion
  251.1 2.6 convolution_convert_fusion.1
  253.7 0.0 reduce-scatter.5.cloned.1.call-update
  253.7 60.1 %reduce-scatter.5.cloned.1.call-done = bf16[256,256]{1,0:T(8,128)(2,1)} async-done(((bf16[4096,256]{1,0:T(8,128)(2,1)}), bf16[256,256]{1,0:T(8,128)(2,1)}) %reduce-scatter.5.cloned.1.call-update) | async-done | bytes 131088 | tf_op jit(solution)/shard_map/reduce_scatter | solution.py:88
  (10 shorter events, 0.0 us)
Async XLA Ops:
  6.5 45.0 %all-gather.2.cloned.1.call-start = ((), (), s32[]{:S(2)}) async-start(), calls=%async_computation.4 | async-start | bytes 2228224 | tf_op jit(solution)/shard_map/all_gather | solution.py:63
  7.3 158.4 %reduce-scatter.3.cloned.1.call-start = ((), (), s32[]{:S(2)}) async-start(), calls=%async_computation.5 | async-start | bytes 15597568 | tf_op jit(solution)/shard_map/reduce_scatter | solution.py:68
  167.0 0.8 copy-start.1
  213.9 6.6 %copy-start.2 = (s32[1,1,6,2]{2,3,1,0:T(2,128)S(1)}, s32[1,1,6,2]{2,3,1,0:T(2,128)}, u32[]{:S(2)}) copy-start(s32[1,1,6,2]{2,3,1,0:T(2,128)} %param.16) | copy-start | bytes 148
  213.9 6.6 %copy-start = (bf16[1,1,6,128,128]{4,3,2,1,0:T(8,128)(2,1)S(1)}, bf16[1,1,6,128,128]{4,3,2,1,0:T(8,128)(2,1)}, u32[]{:S(2)}) copy-start(bf16[1,1,6,128,128]{4,3,2,1,0:T(8,128)(2,1)} %param.14) | copy-start | bytes 589828
  213.9 32.0 %all-to-all-start.1 = ((bf16[16,1,128,512]{2,3,1,0:T(8,128)(2,1)}), bf16[16,1,128,512]{2,3,1,0:T(8,128)(2,1)S(1)}, u32[]{:S(2)}, u32[]{:S(2)}) async-start(bf16[16,1,128,512]{2,3,1,0:T(8,128)(2,1)} %get-tuple-element.6), calls=%async_computation.2 | async-start | bytes 4194304 | tf_op jit(solution)/shard_map/all_to_all | solution.py:35
  219.8 94.0 %reduce-scatter.5.cloned.1.call-start = ((), (), s32[]{:S(2)}) async-start(), calls=%async_computation.6 | async-start | bytes 2228224 | tf_op jit(solution)/shard_map/reduce_scatter | solution.py:88
Sparse Core Ops, SparseCore 0:
  9.2 42.3 all-gather.1
  60.6 105.0 reduce-scatter.2
  253.8 59.8 reduce-scatter.4
where the time goes:
time: 321 us; the launch traced here: 320 us
  waiting for transfers between devices  227 us (71%)
  blocking collectives  31.6 us (10%)
  local copies, waits for them, and re-layouts  23 us (7%)
  matrix products  15.1 us (5%)
  between operations  14.5 us (5%)
  starting transfers between devices  5.92 us (2%)
    reduce_scatter x1, waiting for transfers between devices, body(): lax.psum_scatter(jnp.dot(gathered, dense_pair, preferred_element_type=jnp...  105 us
    reduce_scatter x1, waiting for transfers between devices, body(): lax.psum_scatter(partial_out.astype(jnp.bfloat16), 'gx', scatter_dimensio...  60.1 us
    all_gather x1, waiting for transfers between devices, body(): gathered = lax.all_gather(tokens, 'gx', axis=0, tiled=True)  40.6 us
    all_to_all x1, blocking collectives, cut_exchange(): lax.all_to_all(section, axis, split_axis=0, concat_axis=0, tiled=True)  31.6 us
    all_to_all x1, waiting for transfers between devices, cut_exchange(): lax.all_to_all(section, axis, split_axis=0, concat_axis=0, tiled=True)  20.9 us
    dot_general x1, matrix products, body(): jnp.dot(gathered, dense_pair, preferred_element_type=jnp.float32)  8.91 us
    convert_element_type x1, local copies, waits for them, and re-layouts, body(): outgoing = jnp.einsum('nfk,guf->gnuk', hidden, select_every, preferred_el...  7.47 us
    all_to_all x2, local copies, waits for them, and re-layouts, cut_exchange(): lax.all_to_all(section, axis, split_axis=0, concat_axis=0, tiled=True)  6.51 us
  transfers between devices with their start and end apart: 4, of which 4 were waited for; matrix products, arithmetic and copies ran while one was open for 2% of the time, Pallas kernels for 0%

commit v1 on v0

v1 whole, which is shorter than its diff:
```python
import functools

import jax
import jax.numpy as jnp
from jax import lax
from jax.experimental import pallas as pl
from jax.experimental.pallas import tpu as pltpu
from jax.sharding import PartitionSpec as P

MESH = pl.DeviceIdType.MESH
BLOCK = 128
HALF = 64
NX, NY, NZ = 4, 4, 8
DB, FB = 2, 7
CAP, CAPD = 10, 6
TILE = 256
GU = CAP * BLOCK
DOWN_AT = GU
META_AT = GU + CAPD * HALF
PIECE = META_AT + 16
ROWS_A = 160


def place():
    gx, gy = lax.axis_index("gx"), lax.axis_index("gy")
    return lax.div(gy, NY), lax.rem(gy, NY), lax.div(gx, 2), lax.rem(gx, 2)


def dev(x, y, z, c):
    return (2 * z + c, NY * x + y)


def wrap(v, n):
    return lax.rem(v + n, n)


def rcopy(src, dst, send, recv, to):
    return pltpu.make_async_remote_copy(
        src_ref=src, dst_ref=dst, send_sem=send, recv_sem=recv, device_id=to, device_id_type=MESH
    )


def greet(x, y, z, c, partner_self):
    barrier = pltpu.get_barrier_semaphore()

    def hail(to):
        pl.semaphore_signal(barrier, inc=1, device_id=to, device_id_type=MESH)

    hail(dev(wrap(x + 1, NX), y, z, c))
    hail(dev(wrap(x - 1, NX), y, z, c))
    hail(dev(x, y, wrap(z + 1, NZ), c))
    hail(dev(x, y, wrap(z - 1, NZ), c))
    for dy in range(1, NY):
        for flip in range(2):
            hail(dev(x, wrap(y + dy, NY), z, c if flip == 0 else 1 - c))
    hail(dev(x, y, z, 1 - c))

    @pl.when(jnp.logical_not(partner_self))
    def _():
        hail(dev(lax.div(z, 2), y, 2 * x + c, lax.rem(z, 2)))

    pl.semaphore_wait(barrier, 11 + jnp.where(partner_self, 0, 1))


def spread_kernel(packed, tok, wbuf, xbuf, w_send, w_recv, x_send, x_recv):
    x, y, z, c = place()
    t = 1 - 2 * c
    partner_self = z == 2 * x + c
    partner = dev(lax.div(z, 2), y, 2 * x + c, lax.rem(z, 2))
    greet(x, y, z, c, partner_self)
    sent = []
    count = {"w": 0, "x": 0}

    def go(kind, src, dst, to):
        i = count[kind]
        count[kind] += 1
        send, recv = (w_send, w_recv) if kind == "w" else (x_send, x_recv)
        copy = rcopy(src, dst, send.at[i], recv.at[i], to)
        copy.start()
        sent.append(copy)
        return copy

    count["x"] = 1
    mine = xbuf.at[z, y]
    perm = rcopy(tok, xbuf.at[2 * x + c, y], x_send.at[0], x_recv.at[0], partner)

    @pl.when(partner_self)
    def _():
        pltpu.make_async_copy(tok, mine, x_recv.at[0]).start()

    @pl.when(jnp.logical_not(partner_self))
    def _():
        perm.start()

    count["w"] = 2
    firsts = []
    for h in range(2):
        yd, cd = 2 * c + h, lax.rem(y, 2)
        same = jnp.logical_and(yd == y, cd == c)
        slot = lax.div(y, 2)
        copy = rcopy(packed.at[h], wbuf.at[x, y], w_send.at[h], w_recv.at[slot], dev(x, yd, z, cd))

        @pl.when(same)
        def _(h=h, slot=slot):
            pltpu.make_async_copy(packed.at[h], wbuf.at[x, y], w_recv.at[slot]).start()

        @pl.when(jnp.logical_not(same))
        def _(copy=copy):
            copy.start()

        firsts.append((same, copy))

    events = []

    def at(time, fn):
        events.append((time, len(events), fn))

    def piece(dx, q):
        return wbuf.at[wrap(x + dx * t + NX, NX), c + 2 * q]

    sibling = dev(x, y, z, 1 - c)
    fwd, back = dev(wrap(x + t, NX), y, z, c), dev(wrap(x - t, NX), y, z, c)
    handed = []

    def hand(dx, q):
        handed.append(go("w", piece(dx, q), piece(dx, q), sibling))

    for q in range(2):
        ring = {}

        def first(q=q, ring=ring):
            pltpu.make_async_copy(packed.at[0], wbuf.at[x, c + 2 * q], w_recv.at[q]).wait()
            ring["m1"] = go("w", piece(0, q), piece(0, q), fwd)
            ring["o1"] = go("w", piece(0, q), piece(0, q), back)
            hand(0, q)

        def second(q=q, ring=ring):
            ring["m1"].wait_recv()
            ring["m2"] = go("w", piece(-1, q), piece(-1, q), fwd)
            hand(-1, q)

        def third(q=q, ring=ring):
            ring["o1"].wait_recv()
            hand(1, q)

        def fourth(q=q, ring=ring):
            ring["m2"].wait_recv()
            hand(2, q)

        at(7 + q, first)
        at(16 + 6 * q, second)
        at(18 + 6 * q, third)
        at(29 + 6 * q, fourth)

    rows_a, rows_b = pl.ds(0, ROWS_A), pl.ds(ROWS_A, TILE - ROWS_A)
    z_up, z_down = dev(x, y, wrap(z + t, NZ), c), dev(x, y, wrap(z - t, NZ), c)
    y_up, y_down = dev(x, wrap(y + t, NY), z, c), dev(x, wrap(y - t, NY), z, c)
    tails = []

    def block(dz, dy, rows):
        return xbuf.at[wrap(z + dz * t + NZ, NZ), wrap(y + dy * t + NY, NY), rows]

    def spread_y(dz, time, rows):
        ring = {}
        ring["m1"] = go("x", block(dz, 0, rows), block(dz, 0, rows), y_up)
        ring["o1"] = go("x", block(dz, 0, rows), block(dz, 0, rows), y_down)

        def second():
            ring["m1"].wait_recv()
            ring["m2"] = go("x", block(dz, -1, rows), block(dz, -1, rows), y_up)

        def third():
            ring["o1"].wait_recv()
            ring["m2"].wait_recv()

        return second, third

    def bundle(dz):
        return xbuf.at[wrap(z + dz * t + NZ, NZ), :, rows_b]

    state = {"later": []}

    def run_later(time, pair, tail):
        at2.append((time + 4, pair[0]))
        tail.append((time + 8, pair[1]))

    at2 = []

    def start_a():
        pltpu.make_async_copy(tok, mine, x_recv.at[0]).wait()
        state["up"] = go("x", block(0, 0, rows_a), block(0, 0, rows_a), z_up)
        state["down"] = go("x", block(0, 0, rows_a), block(0, 0, rows_a), z_down)
        state["by"] = spread_y(0, 10, rows_b)
        state["ay0"] = spread_y(0, 10, rows_a)

    at(10, start_a)
    for k in range(1, 5):

        def up(k=k):
            state["up"].wait_recv()
            if k < 4:
                state["up"] = go("x", block(-k, 0, rows_a), block(-k, 0, rows_a), z_up)
            state[f"ay{-k}"] = spread_y(-k, 0, rows_a)

        at(10 + 3 * k, up)
        if k < 4:

            def down(k=k):
                state["down"].wait_recv()
                if k < 3:
                    state["down"] = go("x", block(k, 0, rows_a), block(k, 0, rows_a), z_down)
                state[f"ay{k}"] = spread_y(k, 0, rows_a)

            at(10.5 + 3 * k, down)
    for dz in range(-4, 4):
        base = 10 + 3 * abs(dz)
        at(base + 4, lambda dz=dz: state[f"ay{dz}"][0]())
        at(base + 9, lambda dz=dz: state[f"ay{dz}"][1]())
    at(12.5, lambda: state["by"][0]())

    def start_b():
        state["by"][1]()
        state["bup"] = go("x", bundle(0), bundle(0), z_up)
        state["bdown"] = go("x", bundle(0), bundle(0), z_down)

    at(15.5, start_b)
    for k in range(1, 5):

        def bup(k=k):
            state["bup"].wait_recv()
            if k < 4:
                state["bup"] = go("x", bundle(-k), bundle(-k), z_up)

        at(15.5 + 5.5 * k, bup)
        if k < 4:

            def bdown(k=k):
                state["bdown"].wait_recv()
                if k < 3:
                    state["bdown"] = go("x", bundle(k), bundle(k), z_down)

            at(16 + 5.5 * k, bdown)

    for _, _, fn in sorted(events, key=lambda e: e[:2]):
        fn()
    for copy in handed:
        copy.wait_recv()
    for copy in sent:
        copy.wait_send()
    for same, copy in firsts:

        @pl.when(jnp.logical_not(same))
        def _(copy=copy):
            copy.wait_send()

    @pl.when(jnp.logical_not(partner_self))
    def _():
        perm.wait_send()


def spread(packed, tok):
    vmem = pl.BlockSpec(memory_space=pltpu.VMEM)
    return pl.pallas_call(
        spread_kernel,
        out_shape=(
            jax.ShapeDtypeStruct((NX, NY, PIECE, BLOCK), jnp.bfloat16),
            jax.ShapeDtypeStruct((NZ, NY, TILE, TILE), jnp.bfloat16),
        ),
        in_specs=[vmem, vmem],
        out_specs=(vmem, vmem),
        scratch_shapes=[
            pltpu.SemaphoreType.DMA((18,)),
            pltpu.SemaphoreType.DMA((18,)),
            pltpu.SemaphoreType.DMA((48,)),
            pltpu.SemaphoreType.DMA((48,)),
        ],
        compiler_params=pltpu.CompilerParams(
            collective_id=0, has_side_effects=True, vmem_limit_bytes=40 * 2**20
        ),
    )(packed, tok)


def ffn_kernel(meta, wbuf, xbuf, out, dense, acc, hid, dense_d):
    acc[...] = jnp.zeros_like(acc)

    @pl.loop(0, NX * NY)
    def _(a):
        xa, ya = a // NY, a % NY
        for r in range(DB):
            for h in range(FB):
                idx = meta[a, r * FB + h]
                start = pl.multiple_of(jnp.maximum(idx, 0) * BLOCK, BLOCK)
                blk = wbuf[xa, ya, pl.ds(start, BLOCK), :]
                keep = jnp.where(idx >= 0, 1.0, 0.0).astype(jnp.bfloat16)
                dense[r * BLOCK : (r + 1) * BLOCK, h * BLOCK : (h + 1) * BLOCK] = blk * keep
        for s in range(2):
            acc[s * TILE : (s + 1) * TILE, :] += jnp.dot(
                xbuf[2 * xa + s, ya], dense[...], preferred_element_type=jnp.float32
            )

    low = lax.broadcasted_iota(jnp.int32, (2 * TILE, BLOCK), 1) < HALF
    for pair in range(4):
        v = acc[:, 2 * pair * BLOCK : (2 * pair + 1) * BLOCK]
        one = jax.nn.silu(v) * pltpu.roll(v, HALF, 1)
        if 2 * pair + 1 < FB:
            w = acc[:, (2 * pair + 1) * BLOCK : (2 * pair + 2) * BLOCK]
            two = jax.nn.silu(pltpu.roll(w, HALF, 1)) * w
        else:
            two = jnp.zeros_like(one)
        hid[:, pair * BLOCK : (pair + 1) * BLOCK] = jnp.where(low, one, two).astype(jnp.bfloat16)
    dense_d[FB * HALF :, :] = jnp.zeros((HALF, TILE), jnp.bfloat16)

    @pl.loop(0, NX * NY)
    def _(a):
        xa, ya = a // NY, a % NY
        for h in range(FB):
            for m in range(DB):
                idx = meta[a, DB * FB + h * DB + m]
                start = pl.multiple_of(DOWN_AT + jnp.maximum(idx, 0) * HALF, HALF)
                blk = wbuf[xa, ya, pl.ds(start, HALF), :]
                keep = jnp.where(idx >= 0, 1.0, 0.0).astype(jnp.bfloat16)
                dense_d[h * HALF : (h + 1) * HALF, m * BLOCK : (m + 1) * BLOCK] = blk * keep
        for s in range(2):
            out[2 * xa + s, ya] = jnp.dot(
                hid[s * TILE : (s + 1) * TILE, :], dense_d[...], preferred_element_type=jnp.float32
            ).astype(jnp.bfloat16)


def ffn(meta, wbuf, xbuf):
    vmem = pl.BlockSpec(memory_space=pltpu.VMEM)
    return pl.pallas_call(
        ffn_kernel,
        out_shape=jax.ShapeDtypeStruct((NZ, NY, TILE, TILE), jnp.bfloat16),
        in_specs=[pl.BlockSpec(memory_space=pltpu.SMEM), vmem, vmem],
        out_specs=vmem,
        scratch_shapes=[
            pltpu.VMEM((DB * BLOCK, FB * BLOCK), jnp.bfloat16),
            pltpu.VMEM((2 * TILE, FB * BLOCK), jnp.float32),
            pltpu.VMEM((2 * TILE, 4 * BLOCK), jnp.bfloat16),
            pltpu.VMEM((4 * BLOCK, TILE), jnp.bfloat16),
        ],
        compiler_params=pltpu.CompilerParams(vmem_limit_bytes=40 * 2**20),
    )(meta, wbuf, xbuf)


def f32(v):
    return v.astype(jnp.float32)


def gather_kernel(
    part, out,
    ay_in1, ay_in2, ay_in3, ay_out, ay_sum, az_in, az_out,
    bz_in, bz_out, b_sum, by_in, by_out, final, send_sem, recv_sem,
):
    x, y, z, c = place()
    t = 1 - 2 * c
    partner_self = z == 2 * x + c
    partner = dev(lax.div(z, 2), y, 2 * x + c, lax.rem(z, 2))
    greet(x, y, z, c, partner_self)
    rows_a, rows_b = pl.ds(0, ROWS_A), pl.ds(ROWS_A, TILE - ROWS_A)
    z_up, z_down = dev(x, y, wrap(z + t, NZ), c), dev(x, y, wrap(z - t, NZ), c)
    y_up, y_down = dev(x, wrap(y + t, NY), z, c), dev(x, wrap(y - t, NY), z, c)
    sent = []

    def go(src, dst, to):
        i = len(sent)
        copy = rcopy(src, dst, send_sem.at[i], recv_sem.at[i], to)
        copy.start()
        sent.append(copy)
        return copy

    def zz(dz):
        return wrap(z + dz * t + NZ, NZ)

    def yy(dy):
        return wrap(y + dy * t + NY, NY)

    order = [4, -3, 3, -2, 2, -1, 1, 0]
    first, direct, second = {}, {}, {}
    for i, dz in enumerate(order):
        first[i] = go(part.at[zz(dz), yy(2), rows_a], ay_in1.at[i], y_up)
        direct[i] = go(part.at[zz(dz), yy(-1), rows_a], ay_in3.at[i], y_down)
        if i == 0:
            bup = go(part.at[zz(4), :, rows_b], bz_in.at[0], z_up)
            bdown = go(part.at[zz(-3), :, rows_b], bz_in.at[4], z_down)

    up, down = None, None

    def a_first(i):
        first[i].wait_recv()
        ay_out[i] = (f32(ay_in1[i]) + f32(part[zz(order[i]), yy(1), rows_a])).astype(jnp.bfloat16)
        second[i] = go(ay_out.at[i], ay_in2.at[i], y_up)

    def a_sum(i):
        direct[i].wait_recv()
        second[i].wait_recv()
        total = f32(ay_in2[i]) + f32(ay_in3[i]) + f32(part[zz(order[i]), y, rows_a])
        ay_sum[i] = total.astype(jnp.bfloat16)

    def at_dz(dz):
        return order.index(dz)

    def b_up(k, copy):
        copy.wait_recv()
        if k == 4:
            return None
        bz_out[k - 1] = (f32(bz_in[k - 1]) + f32(part[zz(4 - k), :, rows_b])).astype(jnp.bfloat16)
        return go(bz_out.at[k - 1], bz_in.at[k], z_up)

    def b_down(k, copy):
        copy.wait_recv()
        if k == 3:
            return None
        bz_out[k + 2] = (f32(bz_in[k + 3]) + f32(part[zz(k - 3), :, rows_b])).astype(jnp.bfloat16)
        return go(bz_out.at[k + 2], bz_in.at[k + 4], z_down)

    def a_up(k, copy):
        copy.wait_recv()
        if k == 4:
            return None
        az_out[k - 1] = (f32(az_in[k - 1]) + f32(ay_sum[at_dz(4 - k)])).astype(jnp.bfloat16)
        return go(az_out.at[k - 1], az_in.at[k], z_up)

    def a_down(k, copy):
        copy.wait_recv()
        if k == 3:
            return None
        az_out[k + 2] = (f32(az_in[k + 3]) + f32(ay_sum[at_dz(k - 3)])).astype(jnp.bfloat16)
        return go(az_out.at[k + 2], az_in.at[k + 4], z_down)

    a_first(0)
    a_first(1)
    bup = b_up(1, bup)
    bdown = b_down(1, bdown)
    a_first(2)
    a_first(3)
    a_sum(0)
    up = go(ay_sum.at[0], az_in.at[0], z_up)
    a_sum(1)
    down = go(ay_sum.at[1], az_in.at[4], z_down)
    bup = b_up(2, bup)
    bdown = b_down(2, bdown)
    a_first(4)
    a_first(5)
    a_sum(2)
    a_sum(3)
    up = a_up(1, up)
    down = a_down(1, down)
    bup = b_up(3, bup)
    bdown = b_down(3, bdown)
    a_first(6)
    a_first(7)
    a_sum(4)
    a_sum(5)
    up = a_up(2, up)
    down = a_down(2, down)
    b_up(4, bup)
    b_sum[...] = (f32(bz_in[3]) + f32(bz_in[6]) + f32(part[z, :, rows_b])).astype(jnp.bfloat16)
    b1 = go(b_sum.at[yy(2)], by_in.at[0], y_up)
    b3 = go(b_sum.at[yy(-1)], by_in.at[2], y_down)
    a_sum(6)
    a_sum(7)
    up = a_up(3, up)
    b1.wait_recv()
    by_out[...] = (f32(by_in[0]) + f32(b_sum[yy(1)])).astype(jnp.bfloat16)
    b2 = go(by_out, by_in.at[1], y_up)
    b3.wait_recv()
    b2.wait_recv()
    final[rows_b] = (f32(by_in[1]) + f32(by_in[2]) + f32(b_sum[y])).astype(jnp.bfloat16)
    a_down(3, down)
    a_up(4, up)
    final[rows_a] = (f32(az_in[3]) + f32(az_in[6]) + f32(ay_sum[7])).astype(jnp.bfloat16)
    last = rcopy(final, out, send_sem.at[len(sent)], recv_sem.at[len(sent)], partner)

    @pl.when(partner_self)
    def _():
        here = pltpu.make_async_copy(final, out, recv_sem.at[len(sent)])
        here.start()
        here.wait()

    @pl.when(jnp.logical_not(partner_self))
    def _():
        last.start()
        last.wait_recv()
        last.wait_send()

    for copy in sent:
        copy.wait_send()


def collect(part):
    vmem = pl.BlockSpec(memory_space=pltpu.VMEM)
    rb = TILE - ROWS_A
    sems = 24 + 7 + 7 + 3 + 1
    bf = lambda *s: pltpu.VMEM(s, jnp.bfloat16)
    return pl.pallas_call(
        gather_kernel,
        out_shape=jax.ShapeDtypeStruct((TILE, TILE), jnp.bfloat16),
        in_specs=[vmem],
        out_specs=vmem,
        scratch_shapes=[
            bf(8, ROWS_A, TILE), bf(8, ROWS_A, TILE), bf(8, ROWS_A, TILE), bf(8, ROWS_A, TILE), bf(8, ROWS_A, TILE),
            bf(7, ROWS_A, TILE), bf(5, ROWS_A, TILE),
            bf(7, NY, rb, TILE), bf(5, NY, rb, TILE), bf(NY, rb, TILE), bf(3, rb, TILE), bf(rb, TILE),
            bf(TILE, TILE),
            pltpu.SemaphoreType.DMA((sems,)),
            pltpu.SemaphoreType.DMA((sems,)),
        ],
        compiler_params=pltpu.CompilerParams(
            collective_id=1, has_side_effects=True, vmem_limit_bytes=40 * 2**20
        ),
    )(part)


def where_slot(rows, cols, count, per_col, n):
    slots = jnp.arange(rows.shape[0])
    hit = (rows * per_col + cols)[None, :] == jnp.arange(n)[:, None]
    hit = jnp.logical_and(hit, (slots < count)[None, :])
    return jnp.sum(jnp.where(hit, slots[None, :] + 1, 0), axis=1) - 1


def body(
    tokens, gate_blocks, up_blocks, gate_coords, gate_count,
    down_blocks, down_rows, down_coords, down_count,
):
    gate = gate_blocks[0, 0].reshape(GU, 2, HALF)
    up = up_blocks[0, 0].reshape(GU, 2, HALF)
    both = jnp.concatenate([gate, up], -1).transpose(1, 0, 2)
    down = down_blocks[0, 0].reshape(CAPD, 2, HALF, BLOCK).transpose(1, 0, 2, 3).reshape(2, CAPD * HALF, BLOCK)
    g_at = where_slot(gate_coords[0, 0, :, 0], gate_coords[0, 0, :, 1], gate_count[0, 0], FB, DB * FB)
    rows = lax.dynamic_index_in_dim(down_rows[0], lax.axis_index("gy"), 0, False)
    kept = jnp.sum(jnp.where(down_coords[0, 0, :, :1] == jnp.arange(rows.shape[0])[None, :], rows[None, :], 0), 1)
    d_at = where_slot(kept, down_coords[0, 0, :, 1], down_count[0, 0], DB, DB * FB)
    row = jnp.concatenate([g_at, d_at, jnp.zeros((BLOCK - 28,), jnp.int32)]).astype(jnp.bfloat16)
    meta = jnp.broadcast_to(row, (2, 16, BLOCK))
    packed = jnp.concatenate([both, down, meta], 1)
    wbuf, xbuf = spread(packed, tokens)
    table = wbuf[:, :, META_AT, :32].astype(jnp.int32).reshape(NX * NY, 32)
    return collect(ffn(table, wbuf, xbuf))


def solution(mesh):
    return jax.shard_map(
        body,
        mesh=mesh,
        in_specs=(
            P("gx", "gy"),
            P("gy", "gx", None, None, None),
            P("gy", "gx", None, None, None),
            P("gy", "gx", None, None),
            P("gy", "gx"),
            P("gx", "gy", None, None, None),
            P("gx", None, None),
            P("gx", "gy", None, None),
            P("gx", "gy"),
        ),
        out_specs=P("gx", "gy"),
        check_vma=False,
    )
```

time: 321 us -> 141 us (0.44)
  waiting for transfers between devices: 227 us -> 0 us
  Pallas kernels: 0 us -> 124 us
  blocking collectives: 31.6 us -> 0 us
  matrix products: 15.1 us -> 0 us
  between operations: 14.5 us -> 1.48 us
  local copies, waits for them, and re-layouts: 23 us -> 11.7 us
  starting transfers between devices: 5.92 us -> 0 us
    reduce_scatter x2 -> x0, waiting for transfers between devices: 165 us -> none  [the longest x1 105 us: body(): lax.psum_scatter(jnp.dot(gathered, dense_pair, preferred_element_type=jnp...]
    pallas_call x0 -> x3, Pallas kernels: none -> 124 us  [the longest x1 55.7 us: spread(): pl.pallas_call(spread_kernel, out_shape=(jax.ShapeDtypeStruct((NX, NY, PI...]
    all_gather x1 -> x0, waiting for transfers between devices: 40.6 us -> none  [body(): gathered = lax.all_gather(tokens, 'gx', axis=0, tiled=True)]
    all_to_all x1 -> x0, blocking collectives: 31.6 us -> none  [cut_exchange(): lax.all_to_all(section, axis, split_axis=0, concat_axis=0, tiled=True)]
    all_to_all x1 -> x0, waiting for transfers between devices: 20.9 us -> none  [cut_exchange(): lax.all_to_all(section, axis, split_axis=0, concat_axis=0, tiled=True)]
    dot_general x5 -> x0, matrix products: 15.1 us -> none  [the longest x1 8.91 us: body(): jnp.dot(gathered, dense_pair, preferred_element_type=jnp.float32)]
    convert_element_type x2 -> x0, local copies, waits for them, and re-layouts: 7.74 us -> none  [the longest x1 7.47 us: body(): outgoing = jnp.einsum('nfk,guf->gnuk', hidden, select_every, preferred_el...]
    unnamed x9 -> x13, local copies, waits for them, and re-layouts: 1.09 us -> 8.16 us
  transfers between devices with their start and end apart: 4 -> 0, of which waited for: 4 -> 0; matrix products, arithmetic and copies ran while one was open for 2% -> 0% of each run, Pallas kernels for 0% -> 0%
where the time goes in v1:
time: 141 us; the launch traced here: 139 us
  Pallas kernels  124 us (88%)
  local copies, waits for them, and re-layouts  11.7 us (8%)
  other arithmetic  2.28 us (2%)
  between operations  1.48 us (1%)
    pallas_call x1, Pallas kernels, spread(): pl.pallas_call(spread_kernel, out_shape=(jax.ShapeDtypeStruct((NX, NY, PI...  55.7 us
    pallas_call x1, Pallas kernels, collect(): pl.pallas_call(gather_kernel, out_shape=jax.ShapeDtypeStruct((TILE, TILE)...  50.5 us
    pallas_call x1, Pallas kernels, ffn(): pl.pallas_call(ffn_kernel, out_shape=jax.ShapeDtypeStruct((NZ, NY, TILE,...  17.5 us
    unnamed x13, local copies, waits for them, and re-layouts  8.16 us

profile of v1, /device:TPU:6, one launch (start us, length us, event | category | flops | bytes accessed | tf_op | source)
XLA Modules:
  0.0 139.2 jit_solution(16470265136041626299)
XLA Ops:
  0.0 0.0 copy-start
  0.0 0.0 copy-start.5
  1.4 0.0 copy-done
  1.4 0.2 dynamic-slice_reduce_fusion
  1.6 0.8 add_bitcast_fusion
  2.3 0.7 slice_bitcast_fusion
  3.0 0.1 select_reduce_fusion.2
  3.1 0.1 select_reduce_fusion
  3.2 0.7 bitcast_add_fusion
  3.9 0.1 select_reduce_fusion.1
  4.0 0.1 pad_maximum_fusion.1
  4.1 0.9 copy.20
  5.1 1.3 reshape.51
  6.3 0.1 copy.18
  6.4 0.0 copy-done.5
  6.4 0.3 reshape.52
  6.7 0.1 copy.19
  6.8 0.0 copy-start.4
  6.8 0.4 maximum_bitcast_fusion
  7.2 0.1 pad_maximum_fusion.packed
  7.3 0.5 copy-done.4
  7.7 55.7 %shard_map.91 = (bf16[4,4,1680,128]{3,2,1,0:T(8,128)(2,1)S(1)}, bf16[8,4,256,256]{3,2,1,0:T(8,128)(2,1)S(1)}) custom-call(bf16[2,1680,128]{2,1,0:T(8,128)(2,1)S(1)} %pad_maximum_fusion.packed, bf16[256,256]{1,0:T(8,128)(2,1)S(1)} %copy-done.4), custom_call_target="tpu_custom_call" | custom-call | tf_op jit(solution)/shard_map/pallas_call | solution.py:263
  63.4 0.0 copy-start.2
  63.4 2.1 %copy-done.2 = bf16[8,4,256,256]{3,2,1,0:T(8,128)(2,1)} copy-done((bf16[8,4,256,256]{3,2,1,0:T(8,128)(2,1)}, bf16[8,4,256,256]{3,2,1,0:T(8,128)(2,1)S(1)}, u32[]{:S(2)}) %copy-start.2) | copy-done | bytes 4194328
  65.5 0.0 copy-start.1
  65.5 2.8 %copy-done.1 = bf16[4,4,1680,128]{3,2,1,0:T(8,128)(2,1)} copy-done((bf16[4,4,1680,128]{3,2,1,0:T(8,128)(2,1)}, bf16[4,4,1680,128]{3,2,1,0:T(8,128)(2,1)S(1)}, u32[]{:S(2)}) %copy-start.1) | copy-done | bytes 6881304
  68.3 0.0 copy-start.3
  68.3 2.2 %copy-done.3 = bf16[8,4,256,256]{3,2,1,0:T(8,128)(2,1)S(1)} copy-done((bf16[8,4,256,256]{3,2,1,0:T(8,128)(2,1)S(1)}, bf16[8,4,256,256]{3,2,1,0:T(8,128)(2,1)}, u32[]{:S(2)}) %copy-start.3) | copy-done | bytes 4194328
  70.5 17.5 %shard_map.92.part = bf16[8,4,256,256]{3,2,1,0:T(8,128)(2,1)S(1)} custom-call(s32[16,32]{1,0:T(8,128)S(1)} %bitcast.21, bf16[4,4,1680,128]{3,2,1,0:T(8,128)(2,1)} %copy-done.1, bf16[8,4,256,256]{3,2,1,0:T(8,128)(2,1)S(1)} %copy-done.3), custom_call_target="tpu_custom_call" | custom-call | tf_op jit(solution)/shard_map/pallas_call | solution.py:331
  88.0 50.5 %shard_map.93 = bf16[256,256]{1,0:T(8,128)(2,1)S(1)} custom-call(bf16[8,4,256,256]{3,2,1,0:T(8,128)(2,1)S(1)} %shard_map.92.part), custom_call_target="tpu_custom_call" | custom-call | tf_op jit(solution)/shard_map/pallas_call | solution.py:496
  138.5 0.7 copy.28
  (8 shorter events, 0.1 us)
Async XLA Ops:
  0.0 1.4 copy-start
  0.0 6.4 %copy-start.5 = (bf16[1,1,10,128,128]{4,3,2,1,0:T(8,128)(2,1)S(1)}, bf16[1,1,10,128,128]{4,3,2,1,0:T(8,128)(2,1)}, u32[]{:S(2)}) copy-start(bf16[1,1,10,128,128]{4,3,2,1,0:T(8,128)(2,1)} %param.11) | copy-start | bytes 983044
  6.8 0.9 copy-start.4
  63.4 2.1 %copy-start.2 = (bf16[8,4,256,256]{3,2,1,0:T(8,128)(2,1)}, bf16[8,4,256,256]{3,2,1,0:T(8,128)(2,1)S(1)}, u32[]{:S(2)}) copy-start(bf16[8,4,256,256]{3,2,1,0:T(8,128)(2,1)S(1)} %get-tuple-element.8.xbuf) | copy-start | bytes 12582916
  65.5 2.8 %copy-start.1 = (bf16[4,4,1680,128]{3,2,1,0:T(8,128)(2,1)}, bf16[4,4,1680,128]{3,2,1,0:T(8,128)(2,1)S(1)}, u32[]{:S(2)}) copy-start(bf16[4,4,1680,128]{3,2,1,0:T(8,128)(2,1)S(1)} %get-tuple-element.7.wbuf) | copy-start | bytes 20643844
  68.3 2.2 %copy-start.3 = (bf16[8,4,256,256]{3,2,1,0:T(8,128)(2,1)S(1)}, bf16[8,4,256,256]{3,2,1,0:T(8,128)(2,1)}, u32[]{:S(2)}) copy-start(bf16[8,4,256,256]{3,2,1,0:T(8,128)(2,1)} %copy-done.2) | copy-start | bytes 12582916

commit v2 on v0

v2 whole, which is shorter than its diff:
```python
import jax
import jax.numpy as jnp
from jax import lax
from jax.experimental import pallas as pl
from jax.experimental.pallas import tpu as pltpu
from jax.sharding import PartitionSpec as P

MESH = pl.DeviceIdType.MESH
BLOCK = 128
HALF = 64
NX, NY, NZ = 4, 4, 8
DB, FB = 2, 7
CAP, CAPD = 10, 6
TILE = 256
GU = CAP * BLOCK
DOWN_AT = GU
META_AT = GU + CAPD * HALF
PIECE = META_AT + 16
WIDE = NY * TILE
HID = FB * HALF
ROWS_A = 160


def place():
    gx, gy = lax.axis_index("gx"), lax.axis_index("gy")
    return lax.div(gy, NY), lax.rem(gy, NY), lax.div(gx, 2), lax.rem(gx, 2)


def dev(x, y, z, c):
    return (2 * z + c, NY * x + y)


def wrap(v, n):
    return lax.rem(v + n, n)


def rcopy(src, dst, send, recv, to):
    return pltpu.make_async_remote_copy(
        src_ref=src, dst_ref=dst, send_sem=send, recv_sem=recv, device_id=to, device_id_type=MESH
    )


def hails(x, y, z, c, partner, partner_self):
    barrier = pltpu.get_barrier_semaphore()

    def hail(to):
        pl.semaphore_signal(barrier, inc=1, device_id=to, device_id_type=MESH)

    hail(dev(wrap(x + 1, NX), y, z, c))
    hail(dev(wrap(x - 1, NX), y, z, c))
    hail(dev(x, y, wrap(z + 1, NZ), c))
    hail(dev(x, y, wrap(z - 1, NZ), c))
    for dy in range(1, NY):
        for flip in range(2):
            hail(dev(x, wrap(y + dy, NY), z, c if flip == 0 else 1 - c))
    hail(dev(x, y, z, 1 - c))

    @pl.when(jnp.logical_not(partner_self))
    def _():
        hail(partner)

    return lambda: pl.semaphore_wait(barrier, 11 + jnp.where(partner_self, 0, 1))


def f32(v):
    return v.astype(jnp.float32)


def bf16(v):
    return v.astype(jnp.bfloat16)


E_AT = {0: 0, -1: 1, 1: 2, 2: 3}
ORDER = [4, -3, 3, -2, 2, -1, 1, 0]


def kernel(
    g_coords, g_count, d_rows, d_coords, d_count,
    tok, gate, up, down, out,
    packed, w_own, w_sib, xb, dgu, dd, acc, hid, part,
    ay_in1, ay_in2, ay_in3, ay_out, ay_sum, az_in, az_out,
    bz_in, bz_out, b_sum, by_in, by_out, final, send_sem, recv_sem,
):
    x, y, z, c = place()
    t = 1 - 2 * c
    partner = dev(lax.div(z, 2), y, 2 * x + c, lax.rem(z, 2))
    partner_self = z == 2 * x + c
    remote_partner = jnp.logical_not(partner_self)
    wait_all_here = hails(x, y, z, c, partner, partner_self)
    sibling = dev(x, y, z, 1 - c)
    x_up, x_down = dev(wrap(x + t, NX), y, z, c), dev(wrap(x - t, NX), y, z, c)
    y_up, y_down = dev(x, wrap(y + t, NY), z, c), dev(x, wrap(y - t, NY), z, c)
    z_up, z_down = dev(x, y, wrap(z + t, NZ), c), dev(x, y, wrap(z - t, NZ), c)
    sent, events, used = [], [], [0]

    def sem():
        used[0] += 1
        return used[0] - 1

    def go(src, dst, to):
        i = sem()
        copy = rcopy(src, dst, send_sem.at[i], recv_sem.at[i], to)
        copy.start()
        sent.append(copy)
        return copy

    def at(time, fn):
        events.append((time, len(events), fn))

    def run():
        for _, _, fn in sorted(events, key=lambda e: e[:2]):
            fn()
        events.clear()

    def xx(dx):
        return wrap(x + dx * t + NX, NX)

    def yy(dy):
        return wrap(y + dy * t + NY, NY)

    def zz(dz):
        return wrap(z + dz * t + NZ, NZ)

    def xblock(zi, yi, row, rows):
        start = pl.multiple_of(lax.rem(zi, 2) * TILE + row, 32)
        return xb.at[lax.div(zi, 2), pl.ds(start, rows), pl.ds(pl.multiple_of(yi * TILE, TILE), TILE)]

    low = lax.broadcasted_iota(jnp.int32, (BLOCK, BLOCK), 1) < HALF
    for s in range(CAP):
        g, u = f32(gate[s]), f32(up[s])
        packed[0, s * BLOCK : (s + 1) * BLOCK, :] = bf16(jnp.where(low, g, pltpu.roll(u, HALF, 1)))
        packed[1, s * BLOCK : (s + 1) * BLOCK, :] = bf16(jnp.where(low, pltpu.roll(g, HALF, 1), u))
    for s in range(CAPD):
        for h in range(2):
            packed[h, DOWN_AT + s * HALF : DOWN_AT + (s + 1) * HALF, :] = down[s, h * HALF : (h + 1) * HALF, :]
    slot_row = lax.broadcasted_iota(jnp.int32, (16, BLOCK), 0)
    ids = jnp.full((16, BLOCK), 99, jnp.int32)
    for s in range(CAP):
        spot = jnp.where(s < g_count[0], g_coords[2 * s] * FB + g_coords[2 * s + 1], 99)
        ids = jnp.where(slot_row == s, spot, ids)
    for s in range(CAPD):
        kept = d_rows[(NY * x + y) * 4 + d_coords[2 * s]]
        spot = jnp.where(s < d_count[0], kept * DB + d_coords[2 * s + 1], 99)
        ids = jnp.where(slot_row == CAP + s, spot, ids)
    for h in range(2):
        packed[h, META_AT:PIECE, :] = bf16(f32(ids))

    wait_all_here()

    perm_at = sem()
    mine = xblock(z, y, 0, TILE)
    perm = rcopy(tok, xblock(2 * x + c, y, 0, TILE), send_sem.at[perm_at], recv_sem.at[perm_at], partner)

    @pl.when(partner_self)
    def _():
        pltpu.make_async_copy(tok, mine, recv_sem.at[perm_at]).start()

    @pl.when(remote_partner)
    def _():
        perm.start()

    w1 = [sem(), sem()]
    firsts = []
    slot, land = lax.rem(y, 2), lax.div(y, 2)
    for h in range(2):
        yd = 2 * c + h
        same = jnp.logical_and(yd == y, land == c)
        dst = w_own.at[0, slot]
        copy = rcopy(packed.at[h], dst, send_sem.at[w1[h]], recv_sem.at[w1[0] + slot], dev(x, yd, z, land))

        @pl.when(same)
        def _(h=h, dst=dst):
            pltpu.make_async_copy(packed.at[h], dst, recv_sem.at[w1[0] + slot]).start()

        @pl.when(jnp.logical_not(same))
        def _(copy=copy):
            copy.start()

        firsts.append((same, copy))

    near = lax.rem(y + jnp.where(land == c, 0, 1), 2)
    handed = {}

    def hand(dx, n, q):
        e = -dx if abs(dx) == 1 else dx
        handed[e, n] = go(w_own.at[E_AT[dx], q], w_sib.at[E_AT[e], q], sibling)

    def build(ref, e, ya0):
        @pl.loop(0, 2)
        def _(q):
            ya = ya0 + q
            xa = xx(e)
            names = f32(ref[E_AT[e], q, META_AT:PIECE, :])
            for r in range(DB):
                for h in range(FB):
                    w = jnp.zeros((BLOCK, BLOCK), jnp.bfloat16)
                    for s in range(CAP):
                        hit = names[s : s + 1, :] == float(r * FB + h)
                        w = jnp.where(hit, ref[E_AT[e], q, s * BLOCK : (s + 1) * BLOCK, :], w)
                    row = pl.multiple_of(ya * TILE + r * BLOCK, BLOCK)
                    dgu[xa, pl.ds(row, BLOCK), h * BLOCK : (h + 1) * BLOCK] = w
            for h in range(FB):
                for m in range(DB):
                    w = jnp.zeros((HALF, BLOCK), jnp.bfloat16)
                    for s in range(CAPD):
                        hit = names[CAP + s : CAP + s + 1, :] == float(h * DB + m)
                        at_row = DOWN_AT + s * HALF
                        w = jnp.where(hit, ref[E_AT[e], q, at_row : at_row + HALF, :], w)
                    dd[xa, ya, h * HALF : (h + 1) * HALF, m * BLOCK : (m + 1) * BLOCK] = w

    def build_own(e):
        build(w_own, e, 2 * c)

    def build_sib(e):
        handed[e, 0].wait_recv()
        handed[e, 1].wait_recv()
        build(w_sib, e, 2 * (1 - c))

    for n in range(2):
        q = near if n == 0 else 1 - near
        ring = {}

        def first(n=n, q=q, ring=ring):
            pltpu.make_async_copy(packed.at[0], w_own.at[0, q], recv_sem.at[w1[0] + q]).wait()
            ring["m1"] = go(w_own.at[0, q], w_own.at[1, q], x_up)
            ring["o1"] = go(w_own.at[0, q], w_own.at[2, q], x_down)
            hand(0, n, q)

        def second(n=n, q=q, ring=ring):
            ring["m1"].wait_recv()
            ring["m2"] = go(w_own.at[1, q], w_own.at[3, q], x_up)
            hand(-1, n, q)

        def third(n=n, q=q, ring=ring):
            ring["o1"].wait_recv()
            hand(1, n, q)

        def fourth(n=n, q=q, ring=ring):
            ring["m2"].wait_recv()
            hand(2, n, q)

        at(5 + 7 * n, first)
        at(12 + 8 * n, second)
        at(13 + 8 * n, third)
        at(21 + 8 * n, fourth)
    at(12.1, lambda: build_own(0))
    at(15.1, lambda: build_sib(0))
    at(21.1, lambda: build_own(-1))
    at(21.2, lambda: build_own(1))
    at(24.1, lambda: build_sib(-1))
    at(24.2, lambda: build_sib(1))

    a_part, b_part = (0, ROWS_A), (ROWS_A, TILE - ROWS_A)

    def pass_on(dz, dy, part_rows, to):
        ref = xblock(zz(dz), yy(dy), *part_rows)
        return go(ref, ref, to)

    def along_y(dz, part_rows, time, then=None):
        ring = {}
        ring["m1"] = pass_on(dz, 0, part_rows, y_up)
        ring["o1"] = pass_on(dz, 0, part_rows, y_down)

        def second():
            ring["m1"].wait_recv()
            ring["m2"] = pass_on(dz, -1, part_rows, y_up)
            if then:
                then(-1)

        def third():
            ring["o1"].wait_recv()
            if then:
                then(1)

        def fourth():
            ring["m2"].wait_recv()
            if then:
                then(2)

        return second, third, fourth

    state = {}

    def z_start(dy):
        state["up", dy] = pass_on(0, dy, b_part, z_up)
        state["down", dy] = pass_on(0, dy, b_part, z_down)

    def z_up_step(k, dy):
        state["up", dy].wait_recv()
        if k < 4:
            state["up", dy] = pass_on(-k, dy, b_part, z_up)

    def z_down_step(k, dy):
        state["down", dy].wait_recv()
        if k < 3:
            state["down", dy] = pass_on(k, dy, b_part, z_down)

    def start_tokens():
        pltpu.make_async_copy(tok, mine, recv_sem.at[perm_at]).wait()
        state["up"] = pass_on(0, 0, a_part, z_up)
        state["down"] = pass_on(0, 0, a_part, z_down)
        state["by"] = along_y(0, b_part, 0, z_start)
        z_start(0)
        state["ay", 0] = along_y(0, a_part, 0)

    at(8, start_tokens)
    for k in range(1, 5):

        def a_up(k=k):
            state["up"].wait_recv()
            if k < 4:
                state["up"] = pass_on(-k, 0, a_part, z_up)
            state["ay", -k] = along_y(-k, a_part, 0)

        def a_down(k=k):
            state["down"].wait_recv()
            if k < 3:
                state["down"] = pass_on(k, 0, a_part, z_down)
            state["ay", k] = along_y(k, a_part, 0)

        at(8 + 3 * k, a_up)
        if k < 4:
            at(8.5 + 3 * k, a_down)
    for dz in range(-4, 4):
        base = 8 + 3 * abs(dz)
        at(base + 3.5, lambda dz=dz: state["ay", dz][0]())
        at(base + 4.0, lambda dz=dz: state["ay", dz][1]())
        at(base + 8.5, lambda dz=dz: state["ay", dz][2]())
    at(11, lambda: state["by"][0]())
    at(11.2, lambda: state["by"][1]())
    at(14, lambda: state["by"][2]())
    for dy, begin in ((0, 8), (-1, 11), (1, 11.3), (2, 14)):
        for k in range(1, 5):
            at(begin + 3.3 * k, lambda k=k, dy=dy: z_up_step(k, dy))
            if k < 4:
                at(begin + 0.3 + 3.3 * k, lambda k=k, dy=dy: z_down_step(k, dy))

    def clear():
        acc[...] = jnp.zeros_like(acc)

        @pl.loop(0, NX * NY)
        def _(a):
            dd[lax.div(a, NY), lax.rem(a, NY), HID:, :] = jnp.zeros((2 * TILE - HID, TILE), jnp.bfloat16)

    at(0, clear)

    def multiply(e):
        for s in range(2):
            acc[s * TILE : (s + 1) * TILE, :] += jnp.dot(
                xb[xx(e), s * TILE : (s + 1) * TILE, :], dgu[xx(e)], preferred_element_type=jnp.float32
            )

    at(40, lambda: multiply(0))
    at(41, lambda: multiply(-1))
    at(42, lambda: multiply(1))
    at(43, lambda: build_own(2))
    at(44, lambda: build_sib(2))
    at(45, lambda: multiply(2))
    run()

    wide = lax.broadcasted_iota(jnp.int32, (2 * TILE, BLOCK), 1) < HALF
    for pair in range(4):
        v = acc[:, 2 * pair * BLOCK : (2 * pair + 1) * BLOCK]
        one = jax.nn.silu(v) * pltpu.roll(v, HALF, 1)
        if 2 * pair + 1 < FB:
            w = acc[:, (2 * pair + 1) * BLOCK : (2 * pair + 2) * BLOCK]
            two = jax.nn.silu(pltpu.roll(w, HALF, 1)) * w
        else:
            two = jnp.zeros_like(one)
        hid[:, pair * BLOCK : (pair + 1) * BLOCK] = bf16(jnp.where(wide, one, two))

    rows_a, rows_b = pl.ds(0, ROWS_A), pl.ds(ROWS_A, TILE - ROWS_A)
    DYS = (2, -1, 1, 0)
    first, direct, second = {}, {}, {}

    def project(i):
        dz = ORDER[i]
        zi = zz(dz)
        mine_rows = hid[pl.ds(pl.multiple_of(lax.rem(zi, 2) * TILE, TILE), TILE), :]
        for j, dy in enumerate(DYS):
            part[zi, yy(dy)] = bf16(
                jnp.dot(mine_rows, dd[lax.div(zi, 2), yy(dy)], preferred_element_type=jnp.float32)
            )
            if dy == 2:
                first[i] = go(part.at[zi, yy(2), rows_a], ay_in1.at[i], y_up)
            if dy == -1:
                direct[i] = go(part.at[zi, yy(-1), rows_a], ay_in3.at[i], y_down)
            if dz == 4:
                state["bu", j] = go(part.at[zi, yy(dy), rows_b], bz_in.at[0, j], z_up)
            if dz == -3:
                state["bd", j] = go(part.at[zi, yy(dy), rows_b], bz_in.at[4, j], z_down)

    def a_first(i):
        first[i].wait_recv()
        ay_out[i] = bf16(f32(ay_in1[i]) + f32(part[zz(ORDER[i]), yy(1), rows_a]))
        second[i] = go(ay_out.at[i], ay_in2.at[i], y_up)

    def a_sum(i):
        direct[i].wait_recv()
        second[i].wait_recv()
        ay_sum[i] = bf16(f32(ay_in2[i]) + f32(ay_in3[i]) + f32(part[zz(ORDER[i]), y, rows_a]))
        if ORDER[i] == 4:
            state["au"] = go(ay_sum.at[i], az_in.at[0], z_up)
        if ORDER[i] == -3:
            state["ad"] = go(ay_sum.at[i], az_in.at[4], z_down)

    def chain_a_up(k):
        state["au"].wait_recv()
        if k < 4:
            az_out[k - 1] = bf16(f32(az_in[k - 1]) + f32(ay_sum[ORDER.index(4 - k)]))
            state["au"] = go(az_out.at[k - 1], az_in.at[k], z_up)

    def chain_a_down(k):
        state["ad"].wait_recv()
        if k < 3:
            az_out[k + 2] = bf16(f32(az_in[k + 3]) + f32(ay_sum[ORDER.index(k - 3)]))
            state["ad"] = go(az_out.at[k + 2], az_in.at[k + 4], z_down)

    def chain_b_up(k, j):
        state["bu", j].wait_recv()
        if k < 4:
            bz_out[k - 1, j] = bf16(f32(bz_in[k - 1, j]) + f32(part[zz(4 - k), yy(DYS[j]), rows_b]))
            state["bu", j] = go(bz_out.at[k - 1, j], bz_in.at[k, j], z_up)

    def chain_b_down(k, j):
        state["bd", j].wait_recv()
        if k < 3:
            bz_out[k + 2, j] = bf16(f32(bz_in[k + 3, j]) + f32(part[zz(k - 3), yy(DYS[j]), rows_b]))
            state["bd", j] = go(bz_out.at[k + 2, j], bz_in.at[k + 4, j], z_down)

    def b_end(j):
        b_sum[j] = bf16(f32(bz_in[3, j]) + f32(bz_in[6, j]) + f32(part[z, yy(DYS[j]), rows_b]))
        if j == 0:
            state["by1"] = go(b_sum.at[0], by_in.at[0], y_up)
        if j == 1:
            state["by3"] = go(b_sum.at[1], by_in.at[2], y_down)

    def b_relay():
        state["by1"].wait_recv()
        by_out[...] = bf16(f32(by_in[0]) + f32(b_sum[2]))
        state["by2"] = go(by_out, by_in.at[1], y_up)

    lasts = []

    def deliver(rows):
        i = sem()
        copy = rcopy(final.at[rows], out.at[rows], send_sem.at[i], recv_sem.at[i], partner)
        here = pltpu.make_async_copy(final.at[rows], out.at[rows], recv_sem.at[i])

        @pl.when(partner_self)
        def _():
            here.start()

        @pl.when(remote_partner)
        def _():
            copy.start()

        lasts.append((copy, here))

    def b_last():
        state["by3"].wait_recv()
        state["by2"].wait_recv()
        final[rows_b] = bf16(f32(by_in[1]) + f32(by_in[2]) + f32(b_sum[3]))
        deliver(rows_b)

    def a_last():
        final[rows_a] = bf16(f32(az_in[3]) + f32(az_in[6]) + f32(ay_sum[7]))
        deliver(rows_a)

    for i in range(8):
        at(0.8 * i, lambda i=i: project(i))
        at(3.2 + 2.6 * i, lambda i=i: a_first(i))
        at(6.5 + 2.6 * i, lambda i=i: a_sum(i))
    for j in range(4):
        for k in range(1, 5):
            at(3.5 + 0.7 * j + 5 * (k - 1), lambda k=k, j=j: chain_b_up(k, j))
            if k < 4:
                at(4.5 + 0.7 * j + 5 * (k - 1), lambda k=k, j=j: chain_b_down(k, j))
        at(3.6 + 0.7 * j + 15, lambda j=j: b_end(j))
    at(23, b_relay)
    at(27, b_last)
    for k in range(1, 5):
        at(11.8 + 5.2 * (k - 1), lambda k=k: chain_a_up(k))
        if k < 4:
            at(14.4 + 5.2 * (k - 1), lambda k=k: chain_a_down(k))
    at(28, a_last)
    run()

    for copy in sent:
        copy.wait_send()
    for same, copy in firsts:

        @pl.when(jnp.logical_not(same))
        def _(copy=copy):
            copy.wait_send()

    @pl.when(remote_partner)
    def _():
        perm.wait_send()

    for copy, here in lasts:
        here.wait()

        @pl.when(remote_partner)
        def _(copy=copy):
            copy.wait_send()


SEMS = 170


def body(
    tokens, gate_blocks, up_blocks, gate_coords, gate_count,
    down_blocks, down_rows, down_coords, down_count,
):
    vmem, smem = pl.BlockSpec(memory_space=pltpu.VMEM), pl.BlockSpec(memory_space=pltpu.SMEM)
    rb = TILE - ROWS_A
    bf = lambda *s: pltpu.VMEM(s, jnp.bfloat16)
    return pl.pallas_call(
        kernel,
        out_shape=jax.ShapeDtypeStruct((TILE, TILE), jnp.bfloat16),
        in_specs=[smem] * 5 + [vmem] * 4,
        out_specs=vmem,
        scratch_shapes=[
            bf(2, PIECE, BLOCK), bf(4, 2, PIECE, BLOCK), bf(4, 2, PIECE, BLOCK),
            bf(NX, 2 * TILE, WIDE), bf(NX, WIDE, FB * BLOCK), bf(NX, NY, 2 * TILE, TILE),
            pltpu.VMEM((2 * TILE, FB * BLOCK), jnp.float32), bf(2 * TILE, 2 * TILE),
            bf(NZ, NY, TILE, TILE),
            bf(8, ROWS_A, TILE), bf(8, ROWS_A, TILE), bf(8, ROWS_A, TILE), bf(8, ROWS_A, TILE), bf(8, ROWS_A, TILE),
            bf(7, ROWS_A, TILE), bf(5, ROWS_A, TILE),
            bf(7, NY, rb, TILE), bf(5, NY, rb, TILE), bf(NY, rb, TILE), bf(3, rb, TILE), bf(rb, TILE),
            bf(TILE, TILE),
            pltpu.SemaphoreType.DMA((SEMS,)),
            pltpu.SemaphoreType.DMA((SEMS,)),
        ],
        compiler_params=pltpu.CompilerParams(
            collective_id=0, has_side_effects=True, vmem_limit_bytes=58 * 2**20
        ),
    )(
        gate_coords.reshape(-1), gate_count.reshape(-1), down_rows.reshape(-1),
        down_coords.reshape(-1), down_count.reshape(-1),
        tokens, gate_blocks[0, 0], up_blocks[0, 0], down_blocks[0, 0],
    )


def solution(mesh):
    return jax.shard_map(
        body,
        mesh=mesh,
        in_specs=(
            P("gx", "gy"),
            P("gy", "gx", None, None, None),
            P("gy", "gx", None, None, None),
            P("gy", "gx", None, None),
            P("gy", "gx"),
            P("gx", "gy", None, None, None),
            P("gx", None, None),
            P("gx", "gy", None, None),
            P("gx", "gy"),
        ),
        out_specs=P("gx", "gy"),
        check_vma=False,
    )
```

time: 321 us -> 112 us (0.35)
  waiting for transfers between devices: 227 us -> 0 us
  Pallas kernels: 0 us -> 104 us
  blocking collectives: 31.6 us -> 0 us
  local copies, waits for them, and re-layouts: 23 us -> 4.53 us
  matrix products: 15.1 us -> 0 us
  between operations: 14.5 us -> 1.32 us
  starting transfers between devices: 5.92 us -> 0 us
    reduce_scatter x2 -> x0, waiting for transfers between devices: 165 us -> none  [the longest x1 105 us: body(): lax.psum_scatter(jnp.dot(gathered, dense_pair, preferred_element_type=jnp...]
    pallas_call x0 -> x1, Pallas kernels: none -> 104 us  [body(): pl.pallas_call(kernel, out_shape=jax.ShapeDtypeStruct((TILE, TILE), jnp.b...]
    all_gather x1 -> x0, waiting for transfers between devices: 40.6 us -> none  [body(): gathered = lax.all_gather(tokens, 'gx', axis=0, tiled=True)]
    all_to_all x1 -> x0, blocking collectives: 31.6 us -> none  [cut_exchange(): lax.all_to_all(section, axis, split_axis=0, concat_axis=0, tiled=True)]
    all_to_all x1 -> x0, waiting for transfers between devices: 20.9 us -> none  [cut_exchange(): lax.all_to_all(section, axis, split_axis=0, concat_axis=0, tiled=True)]
    dot_general x5 -> x0, matrix products: 15.1 us -> none  [the longest x1 8.91 us: body(): jnp.dot(gathered, dense_pair, preferred_element_type=jnp.float32)]
    convert_element_type x2 -> x0, local copies, waits for them, and re-layouts: 7.74 us -> none  [the longest x1 7.47 us: body(): outgoing = jnp.einsum('nfk,guf->gnuk', hidden, select_every, preferred_el...]
    all_to_all x2 -> x0, local copies, waits for them, and re-layouts: 6.51 us -> none  [cut_exchange(): lax.all_to_all(section, axis, split_axis=0, concat_axis=0, tiled=True)]
  transfers between devices with their start and end apart: 4 -> 0, of which waited for: 4 -> 0; matrix products, arithmetic and copies ran while one was open for 2% -> 0% of each run, Pallas kernels for 0% -> 0%
where the time goes in v2:
time: 112 us; the launch traced here: 110 us
  Pallas kernels  104 us (93%)
  local copies, waits for them, and re-layouts  4.53 us (4%)
  between operations  1.32 us (1%)
    pallas_call x1, Pallas kernels, body(): pl.pallas_call(kernel, out_shape=jax.ShapeDtypeStruct((TILE, TILE), jnp.b...  104 us
    unnamed x10, local copies, waits for them, and re-layouts  2.66 us

profile of v2, /device:TPU:6, one launch (start us, length us, event | category | flops | bytes accessed | tf_op | source)
XLA Modules:
  0.0 110.1 jit_solution(15717917883118634347)
XLA Ops:
  1.3 0.0 copy-start.1
  1.3 0.7 copy-done.1
  2.0 0.1 copy.15
  2.1 0.0 copy-start.2
  2.1 0.6 reshape.18.d_coords
  2.7 0.1 copy-done.2
  2.8 0.1 copy.13
  2.8 0.0 copy-start
  2.8 0.6 reshape.15.g_coords
  3.4 0.1 copy-done
  3.5 0.1 copy.14
  3.6 0.7 reshape.17.d_rows
  4.3 104.2 %shard_map.91 = bf16[256,256]{1,0:T(8,128)(2,1)} custom-call(s32[20]{0:T(128)} %reshape.15.g_coords, s32[1]{0:T(128)} %bitcast.5.g_count, s32[64]{0:T(128)} %reshape.17.d_rows, s32[12]{0:T(128)} %reshape.18.d_coords, s32[1]{0:T(128)} %bitcast.6.d_count, bf16[256,256]{1,0:T(8,128)(2,1)} %tok.1, bf16[10,128,128]{2,1,0:T(8,128)(2,1)} %bitcast.7, ...), custom_call_target="tpu_custom_call" | custom-call | tf_op jit(solution)/shard_map/pallas_call | solution.py:519
  108.5 1.6 %copy.19 = bf16[256,256]{1,0:T(8,128)(2,1)} copy(bf16[256,256]{1,0:T(8,128)(2,1)} %shard_map.91) | data formatting | bytes 262144
Async XLA Ops:
  1.3 0.7 copy-start.1
  2.1 0.7 copy-start.2
  2.8 0.7 copy-start

commit v3 on v2

--- a/solution.py
+++ b/solution.py
@@ -15,7 +15,8 @@
 GU = CAP * BLOCK
 DOWN_AT = GU
 META_AT = GU + CAPD * HALF
-PIECE = META_AT + 16
+PIECE = META_AT + 32
+PART = PIECE // 2
 WIDE = NY * TILE
 HID = FB * HALF
 ROWS_A = 160
@@ -71,13 +72,13 @@
 
 
 E_AT = {0: 0, -1: 1, 1: 2, 2: 3}
-ORDER = [4, -3, 3, -2, 2, -1, 1, 0]
+ORDER = [4, -2, -3, 3, 2, -1, 1, 0]
 
 
 def kernel(
     g_coords, g_count, d_rows, d_coords, d_count,
     tok, gate, up, down, out,
-    packed, w_own, w_sib, xb, dgu, dd, acc, hid, part,
+    packed, w_all, relayed, xb, dgu, dd, acc, hid, part,
     ay_in1, ay_in2, ay_in3, ay_out, ay_sum, az_in, az_out,
     bz_in, bz_out, b_sum, by_in, by_out, final, send_sem, recv_sem,
 ):
@@ -133,124 +134,146 @@
     for s in range(CAPD):
         for h in range(2):
             packed[h, DOWN_AT + s * HALF : DOWN_AT + (s + 1) * HALF, :] = down[s, h * HALF : (h + 1) * HALF, :]
-    slot_row = lax.broadcasted_iota(jnp.int32, (16, BLOCK), 0)
-    ids = jnp.full((16, BLOCK), 99, jnp.int32)
+    slot_row = lax.broadcasted_iota(jnp.int32, (PIECE - META_AT, BLOCK), 0)
+    ids = jnp.full((PIECE - META_AT, BLOCK), 99, jnp.int32)
     for s in range(CAP):
-        spot = jnp.where(s < g_count[0], g_coords[2 * s] * FB + g_coords[2 * s + 1], 99)
+        spot = jnp.where(s < g_count[0], g_coords[0, s] * FB + g_coords[1, s], 99)
         ids = jnp.where(slot_row == s, spot, ids)
     for s in range(CAPD):
-        kept = d_rows[(NY * x + y) * 4 + d_coords[2 * s]]
-        spot = jnp.where(s < d_count[0], kept * DB + d_coords[2 * s + 1], 99)
+        kept = d_rows[d_coords[0, s], NY * x + y]
+        spot = jnp.where(s < d_count[0], kept * DB + d_coords[1, s], 99)
         ids = jnp.where(slot_row == CAP + s, spot, ids)
     for h in range(2):
         packed[h, META_AT:PIECE, :] = bf16(f32(ids))
 
     wait_all_here()
 
-    perm_at = sem()
-    mine = xblock(z, y, 0, TILE)
-    perm = rcopy(tok, xblock(2 * x + c, y, 0, TILE), send_sem.at[perm_at], recv_sem.at[perm_at], partner)
-
-    @pl.when(partner_self)
-    def _():
-        pltpu.make_async_copy(tok, mine, recv_sem.at[perm_at]).start()
-
-    @pl.when(remote_partner)
-    def _():
-        perm.start()
-
-    w1 = [sem(), sem()]
+    a_part, b_part = (0, ROWS_A), (ROWS_A, TILE - ROWS_A)
+
+    lands = [sem() for _ in range(NY)]
+    relay_at = sem()
     firsts = []
-    slot, land = lax.rem(y, 2), lax.div(y, 2)
+
+    def half(xi, yi, u):
+        start = u * PART if isinstance(u, int) else pl.multiple_of(u * PART, 16)
+        return w_all.at[xi, yi, pl.ds(start, PART)]
+
+    def perm_part(rows):
+        i = sem()
+        src, mine = tok.at[pl.ds(*rows)], xblock(z, y, *rows)
+        copy = rcopy(src, xblock(2 * x + c, y, *rows), send_sem.at[i], recv_sem.at[i], partner)
+        here = pltpu.make_async_copy(src, mine, recv_sem.at[i])
+
+        @pl.when(partner_self)
+        def _():
+            here.start()
+
+        @pl.when(remote_partner)
+        def _():
+            copy.start()
+
+        return copy, here
+
+    perm_b = perm_part(b_part)
     for h in range(2):
         yd = 2 * c + h
-        same = jnp.logical_and(yd == y, land == c)
-        dst = w_own.at[0, slot]
-        copy = rcopy(packed.at[h], dst, send_sem.at[w1[h]], recv_sem.at[w1[0] + slot], dev(x, yd, z, land))
-
-        @pl.when(same)
-        def _(h=h, dst=dst):
-            pltpu.make_async_copy(packed.at[h], dst, recv_sem.at[w1[0] + slot]).start()
-
-        @pl.when(jnp.logical_not(same))
-        def _(copy=copy):
-            copy.start()
-
-        firsts.append((same, copy))
-
-    near = lax.rem(y + jnp.where(land == c, 0, 1), 2)
-    handed = {}
-
-    def hand(dx, n, q):
-        e = -dx if abs(dx) == 1 else dx
-        handed[e, n] = go(w_own.at[E_AT[dx], q], w_sib.at[E_AT[e], q], sibling)
-
-    def build(ref, e, ya0):
-        @pl.loop(0, 2)
-        def _(q):
-            ya = ya0 + q
-            xa = xx(e)
-            names = f32(ref[E_AT[e], q, META_AT:PIECE, :])
-            for r in range(DB):
-                for h in range(FB):
-                    w = jnp.zeros((BLOCK, BLOCK), jnp.bfloat16)
-                    for s in range(CAP):
-                        hit = names[s : s + 1, :] == float(r * FB + h)
-                        w = jnp.where(hit, ref[E_AT[e], q, s * BLOCK : (s + 1) * BLOCK, :], w)
-                    row = pl.multiple_of(ya * TILE + r * BLOCK, BLOCK)
-                    dgu[xa, pl.ds(row, BLOCK), h * BLOCK : (h + 1) * BLOCK] = w
+        far = yd == wrap(y + 2, NY)
+        for u in range(2):
+            i = sem()
+            src = packed.at[h, pl.ds(u * PART, PART)]
+            same = jnp.logical_and(yd == y, c == u)
+            there = rcopy(src, half(x, y, u), send_sem.at[i], recv_sem.at[lands[0] + y], dev(x, yd, z, u))
+            hop = rcopy(src, relayed, send_sem.at[i], recv_sem.at[relay_at], dev(x, wrap(y + 1 - 2 * u, NY), z, u))
+
+            @pl.when(far)
+            def _(hop=hop):
+                hop.start()
+
+            @pl.when(same)
+            def _(src=src, u=u):
+                pltpu.make_async_copy(src, half(x, y, u), recv_sem.at[lands[0] + y]).start()
+
+            @pl.when(jnp.logical_not(jnp.logical_or(far, same)))
+            def _(there=there):
+                there.start()
+
+            firsts.append((same, there))
+    perm_a = perm_part(a_part)
+
+    def relay():
+        pltpu.make_async_copy(relayed, relayed, recv_sem.at[relay_at]).wait()
+        i = sem()
+        copy = rcopy(relayed, half(x, yy(-1), c), send_sem.at[i], recv_sem.at[lands[0] + yy(-1)], y_up)
+        copy.start()
+        sent.append(copy)
+
+    at(RELAY_STEP, relay)
+
+    handed = []
+
+    def hand(dx, dy):
+        ref = half(xx(dx), yy(dy), c)
+        handed.append(go(ref, ref, sibling))
+        handed_at[-dx if abs(dx) == 1 else dx, -dy if abs(dy) == 1 else dy] = handed[-1]
+
+    handed_at = {}
+
+    def build(e, i):
+        if i == 0:
+            for dy in (0, 1, -1, 2):
+                handed_at[e, dy].wait_recv()
+        xa = xx(e)
+
+        names = w_all[xa, i, META_AT : META_AT + 16, :]
+        names = [jnp.broadcast_to(names[s : s + 1, :], (BLOCK, BLOCK)) for s in range(CAP + CAPD)]
+
+        @pl.loop(0, DB)
+        def _(r):
             for h in range(FB):
-                for m in range(DB):
-                    w = jnp.zeros((HALF, BLOCK), jnp.bfloat16)
-                    for s in range(CAPD):
-                        hit = names[CAP + s : CAP + s + 1, :] == float(h * DB + m)
-                        at_row = DOWN_AT + s * HALF
-                        w = jnp.where(hit, ref[E_AT[e], q, at_row : at_row + HALF, :], w)
-                    dd[xa, ya, h * HALF : (h + 1) * HALF, m * BLOCK : (m + 1) * BLOCK] = w
-
-    def build_own(e):
-        build(w_own, e, 2 * c)
-
-    def build_sib(e):
-        handed[e, 0].wait_recv()
-        handed[e, 1].wait_recv()
-        build(w_sib, e, 2 * (1 - c))
-
-    for n in range(2):
-        q = near if n == 0 else 1 - near
+                w = jnp.zeros((BLOCK, BLOCK), jnp.bfloat16)
+                for s in range(CAP):
+                    hit = names[s] == (r * FB + h).astype(jnp.bfloat16)
+                    w = jnp.where(hit, w_all[xa, i, s * BLOCK : (s + 1) * BLOCK, :], w)
+                dgu[xa, pl.ds(pl.multiple_of(i * TILE + r * BLOCK, BLOCK), BLOCK), h * BLOCK : (h + 1) * BLOCK] = w
+
+        for h in range(FB):
+            for m in range(DB):
+                w = jnp.zeros((HALF, BLOCK), jnp.bfloat16)
+                for s in range(CAPD):
+                    hit = names[CAP + s][:HALF] == jnp.bfloat16(h * DB + m)
+                    at_row = DOWN_AT + s * HALF
+                    w = jnp.where(hit, w_all[xa, i, at_row : at_row + HALF, :], w)
+                dd[xa, i, h * HALF : (h + 1) * HALF, m * BLOCK : (m + 1) * BLOCK] = w
+
+    for n, dy in enumerate((0, 1, -1, 2)):
         ring = {}
 
-        def first(n=n, q=q, ring=ring):
-            pltpu.make_async_copy(packed.at[0], w_own.at[0, q], recv_sem.at[w1[0] + q]).wait()
-            ring["m1"] = go(w_own.at[0, q], w_own.at[1, q], x_up)
-            ring["o1"] = go(w_own.at[0, q], w_own.at[2, q], x_down)
-            hand(0, n, q)
-
-        def second(n=n, q=q, ring=ring):
+        def first(dy=dy, ring=ring):
+            pltpu.make_async_copy(relayed, half(x, yy(dy), c), recv_sem.at[lands[0] + yy(dy)]).wait()
+            ring["m1"] = go(half(x, yy(dy), c), half(x, yy(dy), c), x_up)
+            ring["o1"] = go(half(x, yy(dy), c), half(x, yy(dy), c), x_down)
+            hand(0, dy)
+
+        def second(dy=dy, ring=ring):
             ring["m1"].wait_recv()
-            ring["m2"] = go(w_own.at[1, q], w_own.at[3, q], x_up)
-            hand(-1, n, q)
-
-        def third(n=n, q=q, ring=ring):
+            ring["m2"] = go(half(xx(-1), yy(dy), c), half(xx(-1), yy(dy), c), x_up)
+            hand(-1, dy)
+
+        def third(dy=dy, ring=ring):
             ring["o1"].wait_recv()
-            hand(1, n, q)
-
-        def fourth(n=n, q=q, ring=ring):
+            hand(1, dy)
+
+        def fourth(dy=dy, ring=ring):
             ring["m2"].wait_recv()
-            hand(2, n, q)
-
-        at(5 + 7 * n, first)
-        at(12 + 8 * n, second)
-        at(13 + 8 * n, third)
-        at(21 + 8 * n, fourth)
-    at(12.1, lambda: build_own(0))
-    at(15.1, lambda: build_sib(0))
-    at(21.1, lambda: build_own(-1))
-    at(21.2, lambda: build_own(1))
-    at(24.1, lambda: build_sib(-1))
-    at(24.2, lambda: build_sib(1))
-
-    a_part, b_part = (0, ROWS_A), (ROWS_A, TILE - ROWS_A)
+            hand(2, dy)
+
+        at(FIRST_AT[dy], first)
+        at(SECOND_AT[dy], second)
+        at(THIRD_AT[dy], third)
+        at(FOURTH_AT[dy], fourth)
+    for e in (0, -1, 1, 2):
+        for i in range(NY):
+            at(BUILD_AT[e, i], lambda e=e, i=i: build(e, i))
 
     def pass_on(dz, dy, part_rows, to):
         ref = xblock(zz(dz), yy(dy), *part_rows)
@@ -295,22 +318,26 @@
         if k < 3:
             state["down", dy] = pass_on(k, dy, b_part, z_down)
 
-    def start_tokens():
-        pltpu.make_async_copy(tok, mine, recv_sem.at[perm_at]).wait()
+    def start_b():
+        perm_b[1].wait()
+        state["by"] = along_y(0, b_part, 0, z_start)
+        z_start(0)
+
+    def start_a():
+        perm_a[1].wait()
         state["up"] = pass_on(0, 0, a_part, z_up)
         state["down"] = pass_on(0, 0, a_part, z_down)
-        state["by"] = along_y(0, b_part, 0, z_start)
-        z_start(0)
         state["ay", 0] = along_y(0, a_part, 0)
 
-    at(8, start_tokens)
+    at(START_B, start_b)
+    at(START_A, start_a)
     for k in range(1, 5):
 
         def a_up(k=k):
             state["up"].wait_recv()
             if k < 4:
                 state["up"] = pass_on(-k, 0, a_part, z_up)
-            state["ay", -k] = along_y(-k, a_part, 0)
+            state["ay", -k if k < 4 else 4] = along_y(-k, a_part, 0)
 
         def a_down(k=k):
             state["down"].wait_recv()
@@ -318,22 +345,19 @@
                 state["down"] = pass_on(k, 0, a_part, z_down)
             state["ay", k] = along_y(k, a_part, 0)
 
-        at(8 + 3 * k, a_up)
+        at(AUP_AT[k], a_up)
         if k < 4:
-            at(8.5 + 3 * k, a_down)
-    for dz in range(-4, 4):
-        base = 8 + 3 * abs(dz)
-        at(base + 3.5, lambda dz=dz: state["ay", dz][0]())
-        at(base + 4.0, lambda dz=dz: state["ay", dz][1]())
-        at(base + 8.5, lambda dz=dz: state["ay", dz][2]())
-    at(11, lambda: state["by"][0]())
-    at(11.2, lambda: state["by"][1]())
-    at(14, lambda: state["by"][2]())
-    for dy, begin in ((0, 8), (-1, 11), (1, 11.3), (2, 14)):
+            at(ADOWN_AT[k], a_down)
+    for dz in ORDER:
+        for j in range(3):
+            at((AY0_AT, AY1_AT, AY2_AT)[j][dz], lambda dz=dz, j=j: state["ay", dz][j]())
+    for j in range(3):
+        at((BY0_AT, BY1_AT, BY2_AT)[j], lambda j=j: state["by"][j]())
+    for dy in (0, -1, 1, 2):
         for k in range(1, 5):
-            at(begin + 3.3 * k, lambda k=k, dy=dy: z_up_step(k, dy))
+            at(ZUP_AT[k, dy], lambda k=k, dy=dy: z_up_step(k, dy))
             if k < 4:
-                at(begin + 0.3 + 3.3 * k, lambda k=k, dy=dy: z_down_step(k, dy))
+                at(ZDOWN_AT[k, dy], lambda k=k, dy=dy: z_down_step(k, dy))
 
     def clear():
         acc[...] = jnp.zeros_like(acc)
@@ -342,49 +366,47 @@
         def _(a):
             dd[lax.div(a, NY), lax.rem(a, NY), HID:, :] = jnp.zeros((2 * TILE - HID, TILE), jnp.bfloat16)
 
-    at(0, clear)
-
-    def multiply(e):
-        for s in range(2):
-            acc[s * TILE : (s + 1) * TILE, :] += jnp.dot(
-                xb[xx(e), s * TILE : (s + 1) * TILE, :], dgu[xx(e)], preferred_element_type=jnp.float32
-            )
-
-    at(40, lambda: multiply(0))
-    at(41, lambda: multiply(-1))
-    at(42, lambda: multiply(1))
-    at(43, lambda: build_own(2))
-    at(44, lambda: build_sib(2))
-    at(45, lambda: multiply(2))
-    run()
-
-    wide = lax.broadcasted_iota(jnp.int32, (2 * TILE, BLOCK), 1) < HALF
-    for pair in range(4):
-        v = acc[:, 2 * pair * BLOCK : (2 * pair + 1) * BLOCK]
-        one = jax.nn.silu(v) * pltpu.roll(v, HALF, 1)
-        if 2 * pair + 1 < FB:
-            w = acc[:, (2 * pair + 1) * BLOCK : (2 * pair + 2) * BLOCK]
-            two = jax.nn.silu(pltpu.roll(w, HALF, 1)) * w
-        else:
-            two = jnp.zeros_like(one)
-        hid[:, pair * BLOCK : (pair + 1) * BLOCK] = bf16(jnp.where(wide, one, two))
+    at(-1, clear)
+
+    def multiply(dz):
+        xa = lax.div(zz(dz), 2)
+        rows = pl.ds(pl.multiple_of(lax.rem(zz(dz), 2) * TILE, TILE), TILE)
+        acc[rows, :] += jnp.dot(xb[xa, rows, :], dgu[xa], preferred_element_type=jnp.float32)
+
+    for dz in ORDER:
+        at(MUL_AT[dz], lambda dz=dz: multiply(dz))
+    wide = lax.broadcasted_iota(jnp.int32, (TILE, BLOCK), 1) < HALF
+
+    def hide(slice_at):
+        rows = pl.ds(pl.multiple_of(slice_at * TILE, TILE), TILE)
+        for pair in range(4):
+            v = acc[rows, 2 * pair * BLOCK : (2 * pair + 1) * BLOCK]
+            one = jax.nn.silu(v) * pltpu.roll(v, HALF, 1)
+            if 2 * pair + 1 < FB:
+                w = acc[rows, (2 * pair + 1) * BLOCK : (2 * pair + 2) * BLOCK]
+                two = jax.nn.silu(pltpu.roll(w, HALF, 1)) * w
+            else:
+                two = jnp.zeros_like(one)
+            hid[rows, pair * BLOCK : (pair + 1) * BLOCK] = bf16(jnp.where(wide, one, two))
 
     rows_a, rows_b = pl.ds(0, ROWS_A), pl.ds(ROWS_A, TILE - ROWS_A)
     DYS = (2, -1, 1, 0)
     first, direct, second = {}, {}, {}
+
+    def begin(i):
+        zi = zz(ORDER[i])
+        first[i] = go(part.at[zi, yy(2), rows_a], ay_in1.at[i], y_up)
+        direct[i] = go(part.at[zi, yy(-1), rows_a], ay_in3.at[i], y_down)
 
     def project(i):
         dz = ORDER[i]
         zi = zz(dz)
         mine_rows = hid[pl.ds(pl.multiple_of(lax.rem(zi, 2) * TILE, TILE), TILE), :]
-        for j, dy in enumerate(DYS):
+        for dy in DYS:
             part[zi, yy(dy)] = bf16(
                 jnp.dot(mine_rows, dd[lax.div(zi, 2), yy(dy)], preferred_element_type=jnp.float32)
             )
-            if dy == 2:
-                first[i] = go(part.at[zi, yy(2), rows_a], ay_in1.at[i], y_up)
-            if dy == -1:
-                direct[i] = go(part.at[zi, yy(-1), rows_a], ay_in3.at[i], y_down)
+        for j, dy in enumerate(DYS):
             if dz == 4:
                 state["bu", j] = go(part.at[zi, yy(dy), rows_b], bz_in.at[0, j], z_up)
             if dz == -3:
@@ -467,23 +489,43 @@
         final[rows_a] = bf16(f32(az_in[3]) + f32(az_in[6]) + f32(ay_sum[7]))
         deliver(rows_a)
 
+    even_done = max(MUL_AT[dz] for dz in ORDER if dz % 2 == 0)
+
+    def early():
+        hide(lax.rem(z, 2))
+        for i in range(2):
+            project(i)
+            begin(i)
+
+    at(even_done + 0.5, early)
+    last_mul = max(MUL_AT.values())
+    rs = last_mul + 1
+    f, s_at, d = RT["f"], RT["s"], RT["d"]
+    at(rs - 0.5, lambda: hide(lax.rem(z + 1, 2)))
     for i in range(8):
-        at(0.8 * i, lambda i=i: project(i))
-        at(3.2 + 2.6 * i, lambda i=i: a_first(i))
-        at(6.5 + 2.6 * i, lambda i=i: a_sum(i))
+        if i >= 2:
+            at(rs + 4.2 + 0.45 * (i - 2), lambda i=i: project(i))
+            at(rs + max(f + d * (i - 2), 4.2 + 0.45 * (i - 2)) + 0.01, lambda i=i: begin(i))
+        at(rs + f + d * i, lambda i=i: a_first(i))
+        at(rs + s_at + d * i, lambda i=i: a_sum(i))
     for j in range(4):
         for k in range(1, 5):
-            at(3.5 + 0.7 * j + 5 * (k - 1), lambda k=k, j=j: chain_b_up(k, j))
+            up = rs + RT["b"] + 0.7 * j + RT["bd"] * (k - 1)
+            at(up, lambda k=k, j=j: chain_b_up(k, j))
             if k < 4:
-                at(4.5 + 0.7 * j + 5 * (k - 1), lambda k=k, j=j: chain_b_down(k, j))
-        at(3.6 + 0.7 * j + 15, lambda j=j: b_end(j))
-    at(23, b_relay)
-    at(27, b_last)
+                at(up + RT["bx"], lambda k=k, j=j: chain_b_down(k, j))
+        at(up + 0.1, lambda j=j: b_end(j))
+    at(up + RT["y"], b_relay)
+    at(up + 2 * RT["y"], b_last)
+    slot = {dz: rs + s_at + d * i + 0.1 for i, dz in enumerate(ORDER)}
+    up, down = slot[4], slot[-3]
     for k in range(1, 5):
-        at(11.8 + 5.2 * (k - 1), lambda k=k: chain_a_up(k))
+        up = max(slot[4 - k], up + RT["z"])
+        at(up, lambda k=k: chain_a_up(k))
         if k < 4:
-            at(14.4 + 5.2 * (k - 1), lambda k=k: chain_a_down(k))
-    at(28, a_last)
+            down = max(slot[k - 3], down + RT["z"])
+            at(down, lambda k=k: chain_a_down(k))
+    at(max(up, down) + 0.1, a_last)
     run()
 
     for copy in sent:
@@ -496,7 +538,8 @@
 
     @pl.when(remote_partner)
     def _():
-        perm.wait_send()
+        perm_a[0].wait_send()
+        perm_b[0].wait_send()
 
     for copy, here in lasts:
         here.wait()
@@ -506,7 +549,27 @@
             copy.wait_send()
 
 
-SEMS = 170
+SEMS = 200
+START_B = 1
+START_A = 9
+FIRST_AT = {0: 0, 1: 2, -1: 10, 2: 16}
+RELAY_STEP = 3
+SECOND_AT = {0: 4, 1: 18, -1: 43, 2: 50}
+THIRD_AT = {0: 5, 1: 19, -1: 34, 2: 44}
+ZUP_AT = {(1, 0): 6, (2, 0): 12, (1, 1): 14, (1, -1): 22, (3, 0): 28, (2, 1): 30, (2, -1): 38, (1, 2): 40, (3, 1): 42, (3, -1): 52, (2, 2): 55, (3, 2): 64, (4, 0): 82, (4, 1): 83, (4, -1): 84, (4, 2): 85}
+ZDOWN_AT = {(1, 0): 7, (2, 0): 13, (1, 1): 15, (1, -1): 24, (2, 1): 31, (1, 2): 39, (2, -1): 41, (2, 2): 48, (3, 0): 95, (3, 1): 96, (3, -1): 97, (3, 2): 98}
+BY1_AT = 8
+BY0_AT = 11
+AUP_AT = {1: 17, 2: 35, 3: 47, 4: 62}
+ADOWN_AT = {1: 20, 2: 36, 3: 46}
+AY0_AT = {0: 21, -1: 32, 1: 37, -2: 45, 2: 49, 3: 63, -3: 66, 4: 68}
+BY2_AT = 23
+BUILD_AT = {(0, 0): 25, (0, 1): 26, (0, 2): 27, (0, 3): 29, (-1, 0): 51, (-1, 1): 53, (-1, 2): 54, (-1, 3): 56, (1, 0): 57, (1, 1): 58, (1, 2): 60, (1, 3): 61, (2, 0): 69, (2, 1): 70, (2, 2): 71, (2, 3): 72}
+FOURTH_AT = {0: 33, 1: 59, -1: 65, 2: 67}
+AY1_AT = {0: 73, -2: 76, 2: 79, 4: 86, -1: 89, 1: 92, 3: 99, -3: 102}
+AY2_AT = {0: 74, -2: 77, 2: 80, 4: 87, -1: 90, 1: 93, 3: 100, -3: 103}
+MUL_AT = {0: 75, -2: 78, 2: 81, 4: 88, -1: 91, 1: 94, 3: 101, -3: 104}
+RT = {"f": 3.9, "s": 7.0, "d": 2.7, "b": 5.0, "bd": 4.8, "bx": 2.5, "y": 2.7, "z": 2.9}
 
 
 def body(
@@ -522,7 +585,7 @@
         in_specs=[smem] * 5 + [vmem] * 4,
         out_specs=vmem,
         scratch_shapes=[
-            bf(2, PIECE, BLOCK), bf(4, 2, PIECE, BLOCK), bf(4, 2, PIECE, BLOCK),
+            bf(2, PIECE, BLOCK), bf(NX, NY, PIECE, BLOCK), bf(PART, BLOCK),
             bf(NX, 2 * TILE, WIDE), bf(NX, WIDE, FB * BLOCK), bf(NX, NY, 2 * TILE, TILE),
             pltpu.VMEM((2 * TILE, FB * BLOCK), jnp.float32), bf(2 * TILE, 2 * TILE),
             bf(NZ, NY, TILE, TILE),
@@ -537,8 +600,8 @@
             collective_id=0, has_side_effects=True, vmem_limit_bytes=58 * 2**20
         ),
     )(
-        gate_coords.reshape(-1), gate_count.reshape(-1), down_rows.reshape(-1),
-        down_coords.reshape(-1), down_count.reshape(-1),
+        gate_coords[0, 0].T, gate_count.reshape(-1), down_rows[0].T,
+        down_coords[0, 0].T, down_count.reshape(-1),
         tokens, gate_blocks[0, 0], up_blocks[0, 0], down_blocks[0, 0],
     )
 

time: 112 us -> 100 us (0.89)
  Pallas kernels: 104 us -> 95.2 us
  local copies, waits for them, and re-layouts: 4.53 us -> 1.57 us
    pallas_call x1, Pallas kernels: 104 us -> 95.2 us  [body(): pl.pallas_call(kernel, out_shape=jax.ShapeDtypeStruct((TILE, TILE), jnp.b...]
    reshape x3 -> x0, local copies, waits for them, and re-layouts: 1.87 us -> none  [the longest x1 0.67 us: body(): down_rows.reshape(-1)]
    unnamed x10 -> x1, local copies, waits for them, and re-layouts: 2.66 us -> 1.57 us
where the time goes in v3:
time: 100 us; the launch traced here: 98.1 us
  Pallas kernels  95.2 us (95%)
  local copies, waits for them, and re-layouts  1.57 us (2%)
  between operations  1.31 us (1%)
    pallas_call x1, Pallas kernels, body(): pl.pallas_call(kernel, out_shape=jax.ShapeDtypeStruct((TILE, TILE), jnp.b...  95.2 us

profile of v3, /device:TPU:6, one launch (start us, length us, event | category | flops | bytes accessed | tf_op | source)
XLA Modules:
  0.0 98.1 jit_solution(11247036687907028882)
XLA Ops:
  1.3 95.2 %shard_map.91 = bf16[256,256]{1,0:T(8,128)(2,1)} custom-call(s32[2,10]{1,0:T(2,128)} %bitcast.20, s32[1]{0:T(128)} %bitcast.14.g_count, s32[4,16]{1,0:T(4,128)} %bitcast.19, s32[2,6]{1,0:T(2,128)} %bitcast.21, s32[1]{0:T(128)} %bitcast.15.d_count, bf16[256,256]{1,0:T(8,128)(2,1)} %tok.1, bf16[10,128,128]{2,1,0:T(8,128)(2,1)} %bitcast.16, ...), custom_call_target="tpu_custom_call" | custom-call | tf_op jit(solution)/shard_map/pallas_call | solution.py:582
  96.5 1.6 %copy.13 = bf16[256,256]{1,0:T(8,128)(2,1)} copy(bf16[256,256]{1,0:T(8,128)(2,1)} %shard_map.91) | data formatting | bytes 262144

commit v4 on v3

--- a/solution.py
+++ b/solution.py
@@ -41,6 +41,14 @@
     )
 
 
+def z_of(x, c):
+    return lax.rem(2 * x + 3 * c, NZ)
+
+
+def x_of(z):
+    return lax.div(lax.rem(z + 5 * lax.rem(z, 2), NZ), 2)
+
+
 def hails(x, y, z, c, partner, partner_self):
     barrier = pltpu.get_barrier_semaphore()
 
@@ -84,8 +92,8 @@
 ):
     x, y, z, c = place()
     t = 1 - 2 * c
-    partner = dev(lax.div(z, 2), y, 2 * x + c, lax.rem(z, 2))
-    partner_self = z == 2 * x + c
+    partner = dev(x_of(z), y, z_of(x, c), lax.rem(z, 2))
+    partner_self = z == z_of(x, c)
     remote_partner = jnp.logical_not(partner_self)
     wait_all_here = hails(x, y, z, c, partner, partner_self)
     sibling = dev(x, y, z, 1 - c)
@@ -124,7 +132,7 @@
 
     def xblock(zi, yi, row, rows):
         start = pl.multiple_of(lax.rem(zi, 2) * TILE + row, 32)
-        return xb.at[lax.div(zi, 2), pl.ds(start, rows), pl.ds(pl.multiple_of(yi * TILE, TILE), TILE)]
+        return xb.at[x_of(zi), pl.ds(start, rows), pl.ds(pl.multiple_of(yi * TILE, TILE), TILE)]
 
     low = lax.broadcasted_iota(jnp.int32, (BLOCK, BLOCK), 1) < HALF
     for s in range(CAP):
@@ -161,7 +169,7 @@
     def perm_part(rows):
         i = sem()
         src, mine = tok.at[pl.ds(*rows)], xblock(z, y, *rows)
-        copy = rcopy(src, xblock(2 * x + c, y, *rows), send_sem.at[i], recv_sem.at[i], partner)
+        copy = rcopy(src, xblock(z_of(x, c), y, *rows), send_sem.at[i], recv_sem.at[i], partner)
         here = pltpu.make_async_copy(src, mine, recv_sem.at[i])
 
         @pl.when(partner_self)
@@ -218,11 +226,9 @@
 
     handed_at = {}
 
-    def build(e, i):
-        if i == 0:
-            for dy in (0, 1, -1, 2):
-                handed_at[e, dy].wait_recv()
-        xa = xx(e)
+    def build(e, dy):
+        handed_at[e, dy].wait_recv()
+        xa, i = xx(e), yy(dy)
 
         names = w_all[xa, i, META_AT : META_AT + 16, :]
         names = [jnp.broadcast_to(names[s : s + 1, :], (BLOCK, BLOCK)) for s in range(CAP + CAPD)]
@@ -272,7 +278,7 @@
         at(THIRD_AT[dy], third)
         at(FOURTH_AT[dy], fourth)
     for e in (0, -1, 1, 2):
-        for i in range(NY):
+        for i in (0, 1, -1, 2):
             at(BUILD_AT[e, i], lambda e=e, i=i: build(e, i))
 
     def pass_on(dz, dy, part_rows, to):
@@ -369,12 +375,23 @@
     at(-1, clear)
 
     def multiply(dz):
-        xa = lax.div(zz(dz), 2)
+        xa = x_of(zz(dz))
         rows = pl.ds(pl.multiple_of(lax.rem(zz(dz), 2) * TILE, TILE), TILE)
         acc[rows, :] += jnp.dot(xb[xa, rows, :], dgu[xa], preferred_element_type=jnp.float32)
 
+    def multiply_if(dz, last):
+        here = x_of(zz(dz)) == xx(2)
+
+        @pl.when(here if last else jnp.logical_not(here))
+        def _():
+            multiply(dz)
+
     for dz in ORDER:
-        at(MUL_AT[dz], lambda dz=dz: multiply(dz))
+        if dz in (0, -2, 2):
+            at(EARLY_AT[dz], lambda dz=dz: multiply_if(dz, False))
+            at(MUL_AT[dz], lambda dz=dz: multiply_if(dz, True))
+        else:
+            at(MUL_AT[dz], lambda dz=dz: multiply(dz))
     wide = lax.broadcasted_iota(jnp.int32, (TILE, BLOCK), 1) < HALF
 
     def hide(slice_at):
@@ -404,7 +421,7 @@
         mine_rows = hid[pl.ds(pl.multiple_of(lax.rem(zi, 2) * TILE, TILE), TILE), :]
         for dy in DYS:
             part[zi, yy(dy)] = bf16(
-                jnp.dot(mine_rows, dd[lax.div(zi, 2), yy(dy)], preferred_element_type=jnp.float32)
+                jnp.dot(mine_rows, dd[x_of(zi), yy(dy)], preferred_element_type=jnp.float32)
             )
         for j, dy in enumerate(DYS):
             if dz == 4:
@@ -550,25 +567,26 @@
 
 
 SEMS = 200
-START_B = 1
-START_A = 9
-FIRST_AT = {0: 0, 1: 2, -1: 10, 2: 16}
-RELAY_STEP = 3
-SECOND_AT = {0: 4, 1: 18, -1: 43, 2: 50}
-THIRD_AT = {0: 5, 1: 19, -1: 34, 2: 44}
-ZUP_AT = {(1, 0): 6, (2, 0): 12, (1, 1): 14, (1, -1): 22, (3, 0): 28, (2, 1): 30, (2, -1): 38, (1, 2): 40, (3, 1): 42, (3, -1): 52, (2, 2): 55, (3, 2): 64, (4, 0): 82, (4, 1): 83, (4, -1): 84, (4, 2): 85}
-ZDOWN_AT = {(1, 0): 7, (2, 0): 13, (1, 1): 15, (1, -1): 24, (2, 1): 31, (1, 2): 39, (2, -1): 41, (2, 2): 48, (3, 0): 95, (3, 1): 96, (3, -1): 97, (3, 2): 98}
-BY1_AT = 8
-BY0_AT = 11
-AUP_AT = {1: 17, 2: 35, 3: 47, 4: 62}
-ADOWN_AT = {1: 20, 2: 36, 3: 46}
-AY0_AT = {0: 21, -1: 32, 1: 37, -2: 45, 2: 49, 3: 63, -3: 66, 4: 68}
-BY2_AT = 23
-BUILD_AT = {(0, 0): 25, (0, 1): 26, (0, 2): 27, (0, 3): 29, (-1, 0): 51, (-1, 1): 53, (-1, 2): 54, (-1, 3): 56, (1, 0): 57, (1, 1): 58, (1, 2): 60, (1, 3): 61, (2, 0): 69, (2, 1): 70, (2, 2): 71, (2, 3): 72}
-FOURTH_AT = {0: 33, 1: 59, -1: 65, 2: 67}
-AY1_AT = {0: 73, -2: 76, 2: 79, 4: 86, -1: 89, 1: 92, 3: 99, -3: 102}
-AY2_AT = {0: 74, -2: 77, 2: 80, 4: 87, -1: 90, 1: 93, 3: 100, -3: 103}
-MUL_AT = {0: 75, -2: 78, 2: 81, 4: 88, -1: 91, 1: 94, 3: 101, -3: 104}
+START_B = 2
+START_A = 7
+FIRST_AT = {0: 0, 1: 3, -1: 13, 2: 23}
+BUILD_AT = {(0, 0): 1, (1, 0): 11, (-1, 0): 12, (0, -1): 14, (0, 1): 18, (0, 2): 28, (1, -1): 40, (2, 0): 42, (-1, 1): 45, (-1, -1): 53, (1, 1): 55, (-1, 2): 59, (1, 2): 62, (2, -1): 76, (2, 1): 78, (2, 2): 81}
+RELAY_STEP = 4
+ZUP_AT = {(1, 0): 5, (2, 0): 15, (1, 1): 21, (3, 0): 26, (1, -1): 29, (2, 1): 35, (2, -1): 43, (1, 2): 47, (3, 1): 54, (3, -1): 56, (2, 2): 60, (3, 2): 71, (4, 0): 85, (4, -1): 86, (4, 1): 87, (4, 2): 89}
+ZDOWN_AT = {(1, 0): 6, (2, 0): 16, (1, 1): 22, (1, -1): 30, (2, 1): 36, (2, -1): 41, (1, 2): 44, (2, 2): 57, (3, 0): 101, (3, 1): 102, (3, -1): 103, (3, 2): 105}
+SECOND_AT = {0: 8, 1: 24, -1: 51, 2: 58}
+THIRD_AT = {0: 9, 1: 25, -1: 39, 2: 52}
+BY1_AT = 10
+BY0_AT = 17
+AUP_AT = {1: 19, 2: 32, 3: 50, 4: 61}
+ADOWN_AT = {1: 20, 2: 33, 3: 48}
+AY0_AT = {0: 27, -1: 34, 1: 37, -2: 46, 2: 49, 3: 70, -3: 77, 4: 79}
+BY2_AT = 31
+FOURTH_AT = {0: 38, 1: 66, -1: 75, 2: 80}
+AY1_AT = {0: 63, -2: 67, 2: 72, 4: 88, -1: 92, 1: 95, -3: 98, 3: 104}
+AY2_AT = {0: 64, -2: 68, 2: 73, 4: 90, -1: 93, 1: 96, -3: 99, 3: 106}
+EARLY_AT = {0: 65, -2: 69, 2: 74}
+MUL_AT = {0: 82, -2: 83, 2: 84, 4: 91, -1: 94, 1: 97, -3: 100, 3: 107}
 RT = {"f": 3.9, "s": 7.0, "d": 2.7, "b": 5.0, "bd": 4.8, "bx": 2.5, "y": 2.7, "z": 2.9}
 
 

time: 100 us -> 97.1 us (0.971)
  the two profiles are of different devices: /device:TPU:6 before, /device:TPU:1 now
where the time goes in v4:
time: 97.1 us; the launch traced here: 96.9 us
  Pallas kernels  94.1 us (97%)
  local copies, waits for them, and re-layouts  1.57 us (2%)
  between operations  1.31 us (1%)
    pallas_call x1, Pallas kernels, body(): pl.pallas_call(kernel, out_shape=jax.ShapeDtypeStruct((TILE, TILE), jnp.b...  94.1 us

profile of v4, /device:TPU:1, one launch (start us, length us, event | category | flops | bytes accessed | tf_op | source)
XLA Modules:
  0.0 96.9 jit_solution(5741271707917551382)
XLA Ops:
  1.3 94.1 %shard_map.91 = bf16[256,256]{1,0:T(8,128)(2,1)} custom-call(s32[2,10]{1,0:T(2,128)} %bitcast.20, s32[1]{0:T(128)} %bitcast.14.g_count, s32[4,16]{1,0:T(4,128)} %bitcast.19, s32[2,6]{1,0:T(2,128)} %bitcast.21, s32[1]{0:T(128)} %bitcast.15.d_count, bf16[256,256]{1,0:T(8,128)(2,1)} %tok.1, bf16[10,128,128]{2,1,0:T(8,128)(2,1)} %bitcast.16, ...), custom_call_target="tpu_custom_call" | custom-call | tf_op jit(solution)/shard_map/pallas_call | solution.py:600
  95.4 1.6 %copy.13 = bf16[256,256]{1,0:T(8,128)(2,1)} copy(bf16[256,256]{1,0:T(8,128)(2,1)} %shard_map.91) | data formatting | bytes 262144

commit v5 on v4

--- a/solution.py
+++ b/solution.py
@@ -526,11 +526,13 @@
         at(rs + f + d * i, lambda i=i: a_first(i))
         at(rs + s_at + d * i, lambda i=i: a_sum(i))
     for j in range(4):
+        ups = [rs + 5.0 + 0.5 * j] + [rs + b0 + bj * j for b0, bj in RT["up"]]
+        downs = [rs + b0 + bj * j for b0, bj in RT["down"]]
         for k in range(1, 5):
-            up = rs + RT["b"] + 0.7 * j + RT["bd"] * (k - 1)
-            at(up, lambda k=k, j=j: chain_b_up(k, j))
+            at(ups[k - 1], lambda k=k, j=j: chain_b_up(k, j))
             if k < 4:
-                at(up + RT["bx"], lambda k=k, j=j: chain_b_down(k, j))
+                at(downs[k - 1], lambda k=k, j=j: chain_b_down(k, j))
+        up = max(ups[3], downs[2])
         at(up + 0.1, lambda j=j: b_end(j))
     at(up + RT["y"], b_relay)
     at(up + 2 * RT["y"], b_last)
@@ -587,7 +589,7 @@
 AY2_AT = {0: 64, -2: 68, 2: 73, 4: 90, -1: 93, 1: 96, -3: 99, 3: 106}
 EARLY_AT = {0: 65, -2: 69, 2: 74}
 MUL_AT = {0: 82, -2: 83, 2: 84, 4: 91, -1: 94, 1: 97, -3: 100, 3: 107}
-RT = {"f": 3.9, "s": 7.0, "d": 2.7, "b": 5.0, "bd": 4.8, "bx": 2.5, "y": 2.7, "z": 2.9}
+RT = {"f": 3.9, "s": 7.0, "d": 2.7, "y": 2.7, "z": 3.6, "up": ((10.2, 1.0), (15.2, 1.0), (19.6, 0.8)), "down": ((8.4, 1.0), (13.4, 1.0), (18.2, 0.9))}
 
 
 def body(

time: 97.1 us -> 94.9 us (0.977)
  the two profiles are of different devices: /device:TPU:1 before, /device:TPU:6 now
where the time goes in v5:
time: 94.9 us; the launch traced here: 94.8 us
  Pallas kernels  91.9 us (97%)
  local copies, waits for them, and re-layouts  1.57 us (2%)
  between operations  1.31 us (1%)
    pallas_call x1, Pallas kernels, body(): pl.pallas_call(kernel, out_shape=jax.ShapeDtypeStruct((TILE, TILE), jnp.b...  91.9 us

profile of v5, /device:TPU:6, one launch (start us, length us, event | category | flops | bytes accessed | tf_op | source)
XLA Modules:
  0.0 94.8 jit_solution(6999033262602436198)
XLA Ops:
  1.3 91.9 %shard_map.91 = bf16[256,256]{1,0:T(8,128)(2,1)} custom-call(s32[2,10]{1,0:T(2,128)} %bitcast.20, s32[1]{0:T(128)} %bitcast.14.g_count, s32[4,16]{1,0:T(4,128)} %bitcast.19, s32[2,6]{1,0:T(2,128)} %bitcast.21, s32[1]{0:T(128)} %bitcast.15.d_count, bf16[256,256]{1,0:T(8,128)(2,1)} %tok.1, bf16[10,128,128]{2,1,0:T(8,128)(2,1)} %bitcast.16, ...), custom_call_target="tpu_custom_call" | custom-call | tf_op jit(solution)/shard_map/pallas_call | solution.py:602
  93.2 1.6 %copy.13 = bf16[256,256]{1,0:T(8,128)(2,1)} copy(bf16[256,256]{1,0:T(8,128)(2,1)} %shard_map.91) | data formatting | bytes 262144

commit v6 on v5

--- a/solution.py
+++ b/solution.py
@@ -534,8 +534,8 @@
                 at(downs[k - 1], lambda k=k, j=j: chain_b_down(k, j))
         up = max(ups[3], downs[2])
         at(up + 0.1, lambda j=j: b_end(j))
-    at(up + RT["y"], b_relay)
-    at(up + 2 * RT["y"], b_last)
+    at(up + 1.7, b_relay)
+    at(up + 4.5, b_last)
     slot = {dz: rs + s_at + d * i + 0.1 for i, dz in enumerate(ORDER)}
     up, down = slot[4], slot[-3]
     for k in range(1, 5):

time: 94.9 us -> 95.1 us (level)
  no operation moved by 1% of the time
where the time goes in v6:
time: 95.1 us; the launch traced here: 94.4 us
  Pallas kernels  91.5 us (96%)
  local copies, waits for them, and re-layouts  1.57 us (2%)
  between operations  1.31 us (1%)
    pallas_call x1, Pallas kernels, body(): pl.pallas_call(kernel, out_shape=jax.ShapeDtypeStruct((TILE, TILE), jnp.b...  91.5 us

profile of v6, /device:TPU:6, one launch (start us, length us, event | category | flops | bytes accessed | tf_op | source)
XLA Modules:
  0.0 94.4 jit_solution(13696086882490063637)
XLA Ops:
  1.3 91.5 %shard_map.91 = bf16[256,256]{1,0:T(8,128)(2,1)} custom-call(s32[2,10]{1,0:T(2,128)} %bitcast.20, s32[1]{0:T(128)} %bitcast.14.g_count, s32[4,16]{1,0:T(4,128)} %bitcast.19, s32[2,6]{1,0:T(2,128)} %bitcast.21, s32[1]{0:T(128)} %bitcast.15.d_count, bf16[256,256]{1,0:T(8,128)(2,1)} %tok.1, bf16[10,128,128]{2,1,0:T(8,128)(2,1)} %bitcast.16, ...), custom_call_target="tpu_custom_call" | custom-call | tf_op jit(solution)/shard_map/pallas_call | solution.py:602
  92.8 1.6 %copy.13 = bf16[256,256]{1,0:T(8,128)(2,1)} copy(bf16[256,256]{1,0:T(8,128)(2,1)} %shard_map.91) | data formatting | bytes 262144
